TPU v7x, 32 devices: a whole 2x2x4 slice. The times are simulated.
32 devices in a mesh: band: 4 (over y, x), slab: 8 (over z, core).
Axes of the slice: x: 2, y: 2, z: 4, core: 2. Of those that a mesh axis runs over, the one named last changes fastest.
Arguments:
- band_block: float32 [4, 2, 2, 128, 128, 128], P(None, None, None, 'band', 'slab'), may hold values from -24 to 24
- material_grid: int32 [128, 128, 128], P('slab'), may hold values from 0 to 3
- inverse_permittivity: float32 [4], replicated, may hold values from 0.077 to 1
- bloch_index: int32 [1], replicated, may hold values from 0 to 7
Outputs:
- search_block: float32 [4, 2, 2, 128, 128, 128], P(None, None, None, 'band', 'slab')
- correlation: float32 [2, 8, 8], replicated
- projected: float32 [2, 8, 8], replicated
All inputs are finite; a program needn't handle non-finite values.
Results may differ from a plain program's by a relative error of at most 0.00005.
Values sent between devices are 32-bit elements; how exact they have to be, the bound alone decides.
A program may use at most 192 MiB of HBM per device.

v0:
```python
from functools import partial
import math

import jax
import jax.numpy as jnp
from jax import lax
from jax.experimental import pallas as pl
from jax.experimental.pallas import tpu as pltpu
from jax.sharding import PartitionSpec as P

KPOINTS = 8


HIGHEST = lax.Precision.HIGHEST


def axis_values(length, weight, fraction, offset, extent):
    indices = offset + jnp.arange(extent, dtype=jnp.int32)
    signed = jnp.where(indices >= length // 2, indices - length, indices).astype(jnp.float32)
    return 2.0 * math.pi / length * (signed + weight * fraction)


def frame(depth_wave, height_wave, width_wave):
    depth_term = depth_wave[:, None, None]
    height_term = height_wave[None, :, None]
    width_term = width_wave[None, None, :]
    planar = jnp.sqrt(width_term * width_term + height_term * height_term)
    magnitude = jnp.sqrt(planar * planar + depth_term * depth_term)
    grid_shape = magnitude.shape
    primary = [
        jnp.broadcast_to(height_term / planar, grid_shape),
        jnp.broadcast_to(-width_term / planar, grid_shape),
        jnp.zeros(grid_shape, magnitude.dtype),
    ]
    secondary = [
        width_term * depth_term / (magnitude * planar),
        height_term * depth_term / (magnitude * planar),
        -planar / magnitude,
    ]
    return (primary, secondary, magnitude)


def curl_field(block, primary, secondary, magnitude):
    first_comp = block[:, 0]
    second_comp = block[:, 1]
    parts = [
        magnitude * (first_comp * secondary[component] - second_comp * primary[component])
        for component in range(3)
    ]
    return jnp.stack(parts, axis=1).reshape((-1,) + first_comp.shape[1:])


def project_back(spectrum, primary, secondary, magnitude, band_count):
    grouped = spectrum.reshape((band_count, 3) + spectrum.shape[1:])
    along_second = (
        grouped[:, 0] * secondary[0] + grouped[:, 1] * secondary[1] + grouped[:, 2] * secondary[2]
    )
    along_primary = (
        grouped[:, 0] * primary[0] + grouped[:, 1] * primary[1] + grouped[:, 2] * primary[2]
    )
    return jnp.stack([magnitude * along_second, -magnitude * along_primary], axis=1)


def transform(values, target, direction):
    length = values.shape[target]
    indices = jnp.arange(length, dtype=jnp.int32)
    products = indices[:, None] * indices[None, :] % length
    angles = 2.0 * math.pi / length * products.astype(jnp.float32)
    cosine = jnp.cos(angles)
    sine_table = direction * jnp.sin(angles)
    letters = "abc"
    source = letters[target - 2]
    formula = "i" + letters + "," + source + "w" + "->" + "i" + letters.replace(source, "w")
    contract = partial(jnp.einsum, formula, precision=HIGHEST)
    real_part = values[:, 0]
    imaginary = values[:, 1]
    new_real = contract(real_part, cosine) - contract(imaginary, sine_table)
    new_imag = contract(real_part, sine_table) + contract(imaginary, cosine)
    return jnp.stack([new_real, new_imag], axis=1)


def cell_values(material_grid, inverse_permittivity, grid_cells):
    inverse_cells = jnp.zeros(material_grid.shape, jnp.float32)
    for material in range(inverse_permittivity.shape[0]):
        inverse_cells = inverse_cells + jnp.where(
            material_grid == material, inverse_permittivity[material], 0.0
        )
    return inverse_cells / grid_cells


def depth_step(shape):
    depth = shape[3]
    step = depth
    plane = 4 * math.prod(shape[:3]) * math.prod(shape[4:])
    while step % 2 == 0 and step * plane > (1 << 20):
        step //= 2
    return step


def block_spec(shape, step):
    return pl.BlockSpec(shape[:3] + (step,) + shape[4:], lambda d: (0, 0, 0, d, 0, 0))


def gram_kernel(plan, step, *refs):
    *inputs, out = refs
    rows, lanes = inputs[0].shape[4:]

    @pl.when(pl.program_id(0) == 0)
    def _():
        out[...] = jnp.zeros_like(out)

    base = 0
    for (left, left_band), rights in plan:

        def body(depth, sums, left=left, left_band=left_band, rights=rights):
            sums = list(sums)
            for row in range(0, rows, 8):
                for lane in range(0, lanes, 128):
                    tile = (depth, pl.ds(row, 8), pl.ds(lane, 128))
                    for comp in range(2):
                        left_real = inputs[left][(left_band, comp, 0) + tile]
                        left_imag = inputs[left][(left_band, comp, 1) + tile]
                        for place, (right, right_band) in enumerate(rights):
                            right_real = inputs[right][(right_band, comp, 0) + tile]
                            right_imag = inputs[right][(right_band, comp, 1) + tile]
                            sums[2 * place] += left_real * right_real + left_imag * right_imag
                            sums[2 * place + 1] += left_real * right_imag - left_imag * right_real
            return tuple(sums)

        zeros = tuple(jnp.zeros((8, 128), jnp.float32) for _ in range(2 * len(rights)))
        sums = lax.fori_loop(0, step, body, zeros)
        for place, value in enumerate(sums):
            out[base + place] += value
        base += 2 * len(rights)


def gram_sums(arrays, pairs):
    shape = arrays[0].shape
    bands = shape[0]
    step = depth_step(shape)
    plan = []
    for left in sorted({left for left, _ in pairs}):
        for band in range(bands):
            rights = [(r, j) for l, r in pairs if l == left for j in range(bands)]
            plan.append(((left, band), rights))
    count = sum(2 * len(rights) for _, rights in plan)
    cells = math.prod(shape[3:])
    sums = pl.pallas_call(
        partial(gram_kernel, plan, step),
        grid=(shape[3] // step,),
        in_specs=[block_spec(shape, step) for _ in arrays],
        out_specs=pl.BlockSpec((count, 8, 128), lambda d: (0, 0, 0)),
        out_shape=jax.ShapeDtypeStruct((count, 8, 128), jnp.float32),
        cost_estimate=pl.CostEstimate(
            flops=8 * count * cells,
            bytes_accessed=4 * len(arrays) * math.prod(shape),
            transcendentals=0,
        ),
    )(*arrays)
    sums = jnp.sum(sums, axis=(1, 2))
    order = []
    for left in sorted({left for left, _ in pairs}):
        order.append([p for p in pairs if p[0] == left])
    found = {}
    base = 0
    for group in order:
        size = bands * len(group) * bands * 2
        part = sums[base : base + size].reshape(bands, len(group), bands, 2)
        for place, pair in enumerate(group):
            found[pair] = part[:, place]
        base += size
    return [found[pair] for pair in pairs]


def residual_kernel(mixing, block, image, weight, out):
    bands, _, _, step, rows, lanes = block.shape

    @pl.loop(0, step)
    def _(depth):
        for row in range(0, rows, 8):
            for lane in range(0, lanes, 128):
                tile = (depth, pl.ds(row, 8), pl.ds(lane, 128))
                scale = weight[tile]
                for comp in range(2):
                    reals = [block[(i, comp, 0) + tile] for i in range(bands)]
                    imags = [block[(i, comp, 1) + tile] for i in range(bands)]
                    for j in range(bands):
                        real = reals[0] * mixing[0, j] - imags[0] * mixing[bands, j]
                        imag = reals[0] * mixing[bands, j] + imags[0] * mixing[0, j]
                        for i in range(1, bands):
                            real += reals[i] * mixing[i, j] - imags[i] * mixing[bands + i, j]
                            imag += reals[i] * mixing[bands + i, j] + imags[i] * mixing[i, j]
                        out[(j, comp, 0) + tile] = (image[(j, comp, 0) + tile] - real) / scale
                        out[(j, comp, 1) + tile] = (image[(j, comp, 1) + tile] - imag) / scale


def residual_block(block, image, mixing, weight):
    shape = block.shape
    step = depth_step(shape)
    spec = block_spec(shape, step)
    return pl.pallas_call(
        residual_kernel,
        grid=(shape[3] // step,),
        in_specs=[
            pl.BlockSpec(memory_space=pltpu.SMEM),
            spec,
            spec,
            pl.BlockSpec((step,) + shape[4:], lambda d: (d, 0, 0)),
        ],
        out_specs=spec,
        out_shape=jax.ShapeDtypeStruct(shape, jnp.float32),
    )(mixing, block, image, weight)


def sum_over_devices(values):
    flat = jnp.concatenate([value.reshape(-1) for value in values])
    for axis in ("slab", "band"):
        flat = jnp.sum(lax.all_gather(flat, axis), axis=0)
    totals = []
    base = 0
    for value in values:
        totals.append(flat[base : base + value.size].reshape(value.shape))
        base += value.size
    return totals


def shards(band_block, material_grid, inverse_permittivity, bloch_index):
    band_groups = lax.axis_size("band")
    slab_count = lax.axis_size("slab")
    band_count = band_block.shape[0]
    depth_share = band_block.shape[3]
    row_share = band_block.shape[4]
    line_length = band_block.shape[5]
    full_depth = depth_share * band_groups
    full_rows = row_share * slab_count
    grid_cells = full_depth * full_rows * line_length
    fraction = (bloch_index[0].astype(jnp.float32) + 1.0) / KPOINTS
    row_offset = lax.axis_index("slab") * row_share
    depth_offset = lax.axis_index("band") * depth_share
    width_wave = axis_values(line_length, 0.5, fraction, 0, line_length)
    row_wave = axis_values(full_rows, 0.35, fraction, row_offset, row_share)
    point_frame = frame(
        axis_values(full_depth, 0.2, fraction, depth_offset, depth_share), row_wave, width_wave
    )
    inverse_cells = cell_values(material_grid, inverse_permittivity, grid_cells)

    def slab_operator(points):
        gathered = lax.all_to_all(points, "band", split_axis=0, concat_axis=3, tiled=True)
        primary, secondary, magnitude = frame(
            axis_values(full_depth, 0.2, fraction, 0, full_depth), row_wave, width_wave
        )
        curled = curl_field(gathered, primary, secondary, magnitude)
        spectrum = transform(transform(curled, 4, 1.0), 2, 1.0)
        spatial = (
            transform(
                lax.all_to_all(spectrum, "slab", split_axis=2, concat_axis=3, tiled=True), 3, 1.0
            )
            * inverse_cells[None, None]
        )
        returned = lax.all_to_all(
            transform(spatial, 3, -1.0), "slab", split_axis=3, concat_axis=2, tiled=True
        )
        finished = transform(transform(returned, 2, -1.0), 4, -1.0)
        local_image = project_back(finished, primary, secondary, magnitude, gathered.shape[0])
        return lax.all_to_all(local_image, "band", split_axis=3, concat_axis=0, tiled=True)

    def apply_operator(points):
        return slab_operator(points)

    image = apply_operator(band_block)
    (own_sum,) = gram_sums([band_block], [(0, 0)])
    (cross_sum,) = gram_sums([band_block, image], [(0, 1)])
    own_total, cross_total = sum_over_devices([own_sum, cross_sum])
    correlation_real = own_total[..., 0] / grid_cells
    correlation_imag = own_total[..., 1] / grid_cells
    cross_real = cross_total[..., 0] / grid_cells
    cross_imag = cross_total[..., 1] / grid_cells
    system = jnp.concatenate(
        [
            jnp.concatenate([correlation_real, -correlation_imag], 1),
            jnp.concatenate([correlation_imag, correlation_real], 1),
        ],
        0,
    )
    right_side = jnp.concatenate([cross_real, cross_imag], 0)
    factor = jnp.linalg.cholesky(system)
    solution = jax.scipy.linalg.cho_solve((factor, True), right_side)
    magnitude = point_frame[2]
    search_block = residual_block(band_block, image, solution, magnitude * magnitude + 1.0)
    search_image = apply_operator(search_block)
    early = gram_sums([band_block, search_block, image], [(0, 1), (1, 1), (1, 2)])
    late = gram_sums([band_block, search_block, search_image], [(0, 2), (1, 2)])
    totals = [total / grid_cells for total in sum_over_devices(early + late)]
    joint = jnp.concatenate(totals[:2], 0)
    across = jnp.concatenate(totals[3:], 0)
    joint_real, joint_imag = joint[..., 0], joint[..., 1]
    back_real, back_imag = totals[2][..., 0], totals[2][..., 1]
    image_real, image_imag = across[..., 0], across[..., 1]
    upper_real = jnp.concatenate([correlation_real, joint_real[:band_count]], 1)
    lower_real = jnp.concatenate([joint_real[:band_count].T, joint_real[band_count:]], 1)
    upper_imag = jnp.concatenate([correlation_imag, joint_imag[:band_count]], 1)
    lower_imag = jnp.concatenate([-joint_imag[:band_count].T, joint_imag[band_count:]], 1)
    correlation = jnp.stack(
        [
            jnp.concatenate([upper_real, lower_real], 0),
            jnp.concatenate([upper_imag, lower_imag], 0),
        ],
        0,
    )
    top_real = jnp.concatenate([cross_real, image_real[:band_count]], 1)
    bottom_real = jnp.concatenate([back_real, image_real[band_count:]], 1)
    top_imag = jnp.concatenate([cross_imag, image_imag[:band_count]], 1)
    bottom_imag = jnp.concatenate([back_imag, image_imag[band_count:]], 1)
    projected = jnp.stack(
        [jnp.concatenate([top_real, bottom_real], 0), jnp.concatenate([top_imag, bottom_imag], 0)],
        0,
    )
    return (search_block, correlation, projected)


def solution(mesh):
    return jax.shard_map(
        shards,
        mesh=mesh,
        in_specs=(P(None, None, None, "band", "slab", None), P("slab", None, None), P(), P()),
        out_specs=(P(None, None, None, "band", "slab", None), P(), P()),
        check_vma=False,
    )
```

profile of v0, /device:TPU:0, one launch (start us, length us, event | category | flops | bytes accessed | tf_op | source)
XLA Modules:
  0.0 1075.9 jit_solution(14981195007168674051)
XLA Ops:
  0.6 5.2 all-to-all-start
  9.0 45.5 %all-to-all-done = f32[4,2,2,32,16,128]{5,4,3,2,1,0:T(8,128)} async-done(((f32[4,2,2,32,16,128]{5,4,3,2,1,0:T(8,128)}), f32[4,2,2,32,16,128]{5,4,3,2,1,0:T(8,128)}, u32[]{:S(2)}, u32[]{:S(2)}) %all-to-all-start) | async-done | bytes 4194336 | tf_op jit(solution)/shard_map/all_to_all | solution.py:248
  86.2 6.3 copy.170
  92.5 5.4 all-to-all-start.1
  98.6 5.2 add_multiply_fusion.4
  103.8 133.0 %all-to-all-done.1 = f32[3,2,128,16,128]{4,3,0,1,2:T(8,128)} async-done(((f32[3,2,128,16,128]{4,3,0,1,2:T(8,128)}), f32[3,2,128,16,128]{4,3,0,1,2:T(8,128)}, u32[]{:S(2)}, u32[]{:S(2)}) %all-to-all-start.1) | async-done | bytes 6291488 | tf_op jit(solution)/shard_map/all_to_all | solution.py:256
  273.2 141.4 %all_to_all.144 = f32[3,2,16,128,128]{4,2,0,1,3:T(8,128)S(1)} all-to-all(f32[3,2,16,128,128]{4,2,0,1,3:T(8,128)S(1)} %copy.180), channel_id=1, replica_groups=mesh['band'=4,'slab'=8] {'slab'}, dimensions={3} | all-to-all | bytes 12582912 | tf_op jit(solution)/shard_map/all_to_all | solution.py:260
  449.0 5.0 all-to-all-start.3
  456.5 5.4 shard_map.67
  463.9 37.3 %all-to-all-done.3 = f32[1,2,2,128,16,128]{5,4,1,2,0,3:T(8,128)} async-done(((f32[1,2,2,128,16,128]{5,4,1,2,0,3:T(8,128)}), f32[1,2,2,128,16,128]{5,4,1,2,0,3:T(8,128)}, u32[]{:S(2)}, u32[]{:S(2)}) %all-to-all-start.3) | async-done | bytes 4194336 | tf_op jit(solution)/shard_map/all_to_all | solution.py:265
  501.2 4.6 copy.307
  505.9 6.2 shard_map.68
  513.5 14.3 %all-reduce = f32[512]{0:T(512)S(1)} all-reduce(f32[512]{0:T(512)S(1)} %maximum_dynamic-update-slice_fusion.1), channel_id=2, replica_groups=mesh['band'=4,'slab'=8] {'slab'}, use_global_device_ids=true, to_apply=%add | all-reduce | flops 512 | bytes 4096
  528.1 8.9 all-reduce.1
  541.8 7.0 shard_map.69.refs_1_
  548.8 49.2 %all_to_all.145 = f32[4,2,2,32,16,128]{5,4,3,2,1,0:T(8,128)S(1)} all-to-all(f32[4,2,2,32,16,128]{5,4,3,2,1,0:T(8,128)} %shard_map.69.refs_1_), channel_id=1, replica_groups=mesh['band'=4,'slab'=8] {'band'}, dimensions={0} | all-to-all | bytes 8388608 | tf_op jit(solution)/shard_map/all_to_all | solution.py:248
  631.6 141.4 %all_to_all.146 = f32[3,2,128,16,128]{4,3,0,1,2:T(8,128)S(1)} all-to-all(f32[3,2,128,16,128]{4,3,0,1,2:T(8,128)S(1)} %copy.203), channel_id=1, replica_groups=mesh['band'=4,'slab'=8] {'slab'}, dimensions={2} | all-to-all | bytes 12582912 | tf_op jit(solution)/shard_map/all_to_all | solution.py:256
  805.8 141.4 %all_to_all.147 = f32[3,2,16,128,128]{4,2,0,1,3:T(8,128)S(1)} all-to-all(f32[3,2,16,128,128]{4,2,0,1,3:T(8,128)S(1)} %copy.213), channel_id=1, replica_groups=mesh['band'=4,'slab'=8] {'slab'}, dimensions={3} | all-to-all | bytes 12582912 | tf_op jit(solution)/shard_map/all_to_all | solution.py:260
  981.1 4.8 all-to-all-start.7
  987.3 11.1 %shard_map.70 = f32[96,8,128]{2,1,0:T(8,128)} custom-call(f32[4,2,2,32,16,128]{5,4,3,2,1,0:T(8,128)} %refs_0_.7, f32[4,2,2,32,16,128]{5,4,3,2,1,0:T(8,128)} %shard_map.69.refs_1_, f32[4,2,2,32,16,128]{5,4,3,2,1,0:T(8,128)} %bitcast.408), custom_call_target="tpu_custom_call" | custom-call | flops 50331648 | bytes 12582912 | tf_op jit(solution)/shard_map/pallas_call | solution.py:148
  1000.6 32.7 %all-to-all-done.7 = f32[1,2,2,128,16,128]{5,4,1,2,0,3:T(8,128)} async-done(((f32[1,2,2,128,16,128]{5,4,1,2,0,3:T(8,128)}), f32[1,2,2,128,16,128]{5,4,1,2,0,3:T(8,128)}, u32[]{:S(2)}, u32[]{:S(2)}) %all-to-all-start.7) | async-done | bytes 4194336 | tf_op jit(solution)/shard_map/all_to_all | solution.py:265
  1037.9 9.1 shard_map.71
  1048.7 14.5 %all-reduce.2 = f32[1280]{0:T(1024)S(1)} all-reduce(f32[1280]{0:T(1024)S(1)} %maximum_dynamic-update-slice_fusion), channel_id=4, replica_groups=mesh['band'=4,'slab'=8] {'slab'}, use_global_device_ids=true, to_apply=%add.2 | all-reduce | flops 1280 | bytes 10240
  1063.6 8.9 all-reduce.3
  (173 shorter events, 227.1 us)
Async XLA Ops:
  0.6 53.8 %all-to-all-start = ((f32[4,2,2,32,16,128]{5,4,3,2,1,0:T(8,128)}), f32[4,2,2,32,16,128]{5,4,3,2,1,0:T(8,128)}, u32[]{:S(2)}, u32[]{:S(2)}) async-start(f32[4,2,2,32,16,128]{5,4,3,2,1,0:T(8,128)} %refs_0_.7), calls=%async_computation | async-start | bytes 8388608 | tf_op jit(solution)/shard_map/all_to_all | solution.py:248
  54.5 3.6 copy-start
  92.5 5.4 copy-start.7
  92.5 144.2 %all-to-all-start.1 = ((f32[3,2,128,16,128]{4,3,0,1,2:T(8,128)}), f32[3,2,128,16,128]{4,3,0,1,2:T(8,128)}, u32[]{:S(2)}, u32[]{:S(2)}) async-start(f32[3,2,128,16,128]{4,3,0,1,2:T(8,128)} %copy.170), calls=%async_computation.1 | async-start | bytes 12582912 | tf_op jit(solution)/shard_map/all_to_all | solution.py:256
  250.3 3.8 copy-start.5
  441.2 1.2 copy-start.1
  441.2 1.5 copy-start.3
  448.9 5.0 copy-start.9
  449.0 5.6 copy-start.8
  449.0 52.3 %all-to-all-start.3 = ((f32[1,2,2,128,16,128]{5,4,1,2,0,3:T(8,128)}), f32[1,2,2,128,16,128]{5,4,1,2,0,3:T(8,128)}, u32[]{:S(2)}, u32[]{:S(2)}) async-start(f32[1,2,2,128,16,128]{5,4,1,2,0,3:T(8,128)} %copy.186), calls=%async_computation.3 | async-start | bytes 8388608 | tf_op jit(solution)/shard_map/all_to_all | solution.py:265
  598.3 1.2 copy-start.2
  783.7 3.9 copy-start.6
  973.8 1.2 copy-start.4
  981.1 52.2 %all-to-all-start.7 = ((f32[1,2,2,128,16,128]{5,4,1,2,0,3:T(8,128)}), f32[1,2,2,128,16,128]{5,4,1,2,0,3:T(8,128)}, u32[]{:S(2)}, u32[]{:S(2)}) async-start(f32[1,2,2,128,16,128]{5,4,1,2,0,3:T(8,128)} %copy.219), calls=%async_computation.7 | async-start | bytes 8388608 | tf_op jit(solution)/shard_map/all_to_all | solution.py:265
where the time goes:
time: 1090 us; the launch traced here: 1080 us
  blocking collectives  520 us (48%)
  waiting for transfers between devices  248 us (23%)
  matrix products  157 us (14%)
  local copies, waits for them, and re-layouts  54 us (5%)
  Pallas kernels  38.9 us (4%)
  other arithmetic  32.5 us (3%)
  starting transfers between devices  20.4 us (2%)
    all_to_all x2, blocking collectives, slab_operator(): lax.all_to_all(transform(spatial, 3, -1.0), 'slab', split_axis=3, concat_...  283 us
    all_to_all x1, blocking collectives, slab_operator(): lax.all_to_all(spectrum, 'slab', split_axis=2, concat_axis=3, tiled=True)  141 us
    all_to_all x1, waiting for transfers between devices, slab_operator(): lax.all_to_all(spectrum, 'slab', split_axis=2, concat_axis=3, tiled=True)  133 us
    dot_general x24, matrix products, transform(): new_real = contract(real_part, cosine) - contract(imaginary, sine_table)  77.9 us
    dot_general x24, matrix products, transform(): new_imag = contract(real_part, sine_table) + contract(imaginary, cosine)  77.9 us
    all_to_all x2, waiting for transfers between devices, slab_operator(): lax.all_to_all(local_image, 'band', split_axis=3, concat_axis=0, tiled=True)  70 us
    all_to_all x1, blocking collectives, slab_operator(): lax.all_to_all(points, 'band', split_axis=0, concat_axis=3, tiled=True)  49.2 us
    unnamed x4, blocking collectives  46.6 us
  transfers between devices with their start and end apart: 4, of which 4 were waited for; matrix products, arithmetic and copies ran while one was open for 1% of the time, Pallas kernels for 2%

commit v1 on v0

v1 whole, which is shorter than its diff:
```python
from functools import partial
import math

import jax
import jax.numpy as jnp
import numpy as np
from jax import lax
from jax.experimental import pallas as pl
from jax.experimental.pallas import tpu as pltpu
from jax.sharding import PartitionSpec as P

KPOINTS = 8
HIGHEST = lax.Precision.HIGHEST
MESH = pl.DeviceIdType.MESH
VMEM_LIMIT = 60 * 1024 * 1024


def axis_values(length, weight, fraction, offset, extent):
    indices = offset + jnp.arange(extent, dtype=jnp.int32)
    signed = jnp.where(indices >= length // 2, indices - length, indices).astype(jnp.float32)
    return 2.0 * math.pi / length * (signed + weight * fraction)


def halves(values):
    high = values.astype(jnp.bfloat16)
    return high, (values - high.astype(jnp.float32)).astype(jnp.bfloat16)


def dft_matrix(length, direction):
    indices = np.arange(length)
    angles = 2.0 * np.pi / length * (np.outer(indices, indices) % length)
    cosine, sine = np.cos(angles), direction * np.sin(angles)
    return np.block([[cosine, -sine], [sine, cosine]])


def numpy_halves(matrix):
    single = matrix.astype(np.float32)
    high = single.astype(jnp.bfloat16)
    low = (single - high.astype(np.float32)).astype(jnp.bfloat16)
    return high, low


def left_table(length, direction):
    return np.concatenate(numpy_halves(dft_matrix(length, direction)), 0)


def right_table(matrix):
    high, low = numpy_halves(matrix)
    return np.concatenate([high, high, low], 0)


def dot(left, right):
    return jnp.dot(left, right, preferred_element_type=jnp.float32)


def left_transform(table, values):
    size = values.shape[0]
    high, low = halves(values)
    main = dot(table[...], high)
    rest = dot(table[:size, :], low)
    return main[:size] + (main[size:] + rest)


def right_transform(values, table):
    high, low = halves(values)
    return dot(jnp.concatenate([high, low, high], 1), table[...])


def step_count(size):
    return 2 if size % 2 == 0 else 1


def gram(acc, base, hermitian, left, right, count, depth_of):
    bands, rows, lanes = left.shape[0], left.shape[4], left.shape[5]
    for i in range(bands):
        others = list(range(i if hermitian else 0, bands))

        def body(step, sums, i=i, others=others):
            depth = depth_of(step)
            sums = list(sums)
            for row in range(0, rows, 8):
                tile = (depth, pl.ds(row, 8), slice(None))
                for comp in range(2):
                    left_real = left[(i, comp, 0) + tile]
                    left_imag = left[(i, comp, 1) + tile]
                    for place, j in enumerate(others):
                        right_real = right[(j, comp, 0) + tile]
                        right_imag = right[(j, comp, 1) + tile]
                        sums[2 * place] += left_real * right_real + left_imag * right_imag
                        sums[2 * place + 1] += left_real * right_imag - left_imag * right_real
            return tuple(sums)

        zeros = tuple(jnp.zeros((8, lanes), jnp.float32) for _ in range(2 * len(others)))
        sums = lax.fori_loop(0, count, body, zeros)
        for place, value in enumerate(sums):
            acc[base + place] += value
        base += 2 * len(others)
    return base


def gram_rows(bands, hermitian):
    return bands * (bands + 1) if hermitian else 2 * bands * bands


def unpack(flat, bands, hermitian):
    real = [[None] * bands for _ in range(bands)]
    imag = [[None] * bands for _ in range(bands)]
    place = 0
    for i in range(bands):
        for j in range(i if hermitian else 0, bands):
            real[i][j], imag[i][j] = flat[place], flat[place + 1]
            if hermitian and j > i:
                real[j][i], imag[j][i] = flat[place], -flat[place + 1]
            place += 2
    stack = lambda rows: jnp.stack([jnp.stack(row) for row in rows])
    return stack(real), stack(imag)


class Place:
    def __init__(self, groups, slabs):
        self.groups, self.slabs = groups, slabs
        self.group = lax.axis_index("band")
        self.slab = lax.axis_index("slab")
        self.layer, self.core = self.slab // 2, self.slab % 2
        self.cell = 2 * self.group + self.core

    def slab_peer(self, step):
        slab = lax.rem(self.slab + step, self.slabs)
        return slab, (self.group, slab)

    def band_peer(self, step):
        group = lax.rem(self.group + step, self.groups)
        return group, (group, self.slab)

    def plane_peer(self, step):
        cell = lax.rem(self.cell + step, 2 * self.groups)
        return cell, (cell // 2, 2 * self.layer + cell % 2)


def enter(devices):
    barrier = pltpu.get_barrier_semaphore()
    for device in devices:
        pl.semaphore_signal(barrier, inc=1, device_id=device, device_id_type=MESH)
    pl.semaphore_wait(barrier, len(devices))


def send(source, target, send_sem, recv_sem, device):
    pltpu.make_async_remote_copy(
        src_ref=source,
        dst_ref=target,
        send_sem=send_sem,
        recv_sem=recv_sem,
        device_id=device,
        device_id_type=MESH,
    ).start()


def await_bytes(ref, sem):
    pltpu.make_async_copy(ref, ref, sem).wait()


def total(place, mine, first, second, sems, values):
    mine[0] = values
    first[place.slab] = values
    for step in range(1, place.slabs):
        _, device = place.slab_peer(step)
        send(mine.at[0], first.at[place.slab], sems.at[0], sems.at[1], device)
    await_bytes(first.at[pl.ds(0, place.slabs - 1)], sems.at[1])
    values = first[0]
    for slab in range(1, place.slabs):
        values = values + first[slab]
    mine[1] = values
    second[place.group] = values
    for step in range(1, place.groups):
        _, device = place.band_peer(step)
        send(mine.at[1], second.at[place.group], sems.at[2], sems.at[3], device)
    await_bytes(second.at[pl.ds(0, place.groups - 1)], sems.at[3])
    values = second[0]
    for group in range(1, place.groups):
        values = values + second[group]
    await_bytes(first.at[pl.ds(0, place.slabs - 1)], sems.at[0])
    await_bytes(second.at[pl.ds(0, place.groups - 1)], sems.at[2])
    return values


def lane_sums(tile, acc):
    rows = acc.shape[0]
    tile[...] = jnp.zeros_like(tile)
    tile[:rows, :] = jnp.sum(acc[...], axis=1)
    ones = jnp.ones((8, tile.shape[1]), jnp.float32)
    return lax.dot_general(
        ones, tile[...], (((1,), (1,)), ((), ())), precision=HIGHEST,
        preferred_element_type=jnp.float32,
    )


def first_kernel(
    groups, slabs, block, waves, depths, cells, x_plus, y_plus, z_plus, z_minus, y_minus, x_minus,
    image, sums, work, out_y, in_z, out_z, in_y, eta, acc, tile, mine, first, second, sems, tail,
):
    place = Place(groups, slabs)
    bands, _, _, depth, rows, width = block.shape
    half = depth // 2
    height = rows * slabs
    length = depth * groups
    share = out_y.shape[3] // half
    step = step_count(half)
    chunks = half // step
    part = step * share

    enter(
        [place.slab_peer(i)[1] for i in range(1, slabs)]
        + [
            (lax.rem(place.group + i, groups), 2 * place.layer + core)
            for i in range(1, groups)
            for core in range(2)
        ]
    )

    @pl.loop(0, chunks)
    def _(k):
        for i in range(1, slabs):
            slab, device = place.slab_peer(i)
            send(
                block.at[slab // 2, :, :, pl.ds(half * (slab % 2) + k * step, step), :, :],
                work.at[:, :, pl.ds(k * step, step), pl.ds(rows * place.slab, rows), :],
                sems.at[0, k], sems.at[1, k], device,
            )

    slab_cells = cells.shape[1]
    for i in range(1, slabs):
        slab, device = place.slab_peer(i)
        send(
            cells.at[2 * place.group + slab % 2],
            eta.at[pl.ds(slab_cells * place.slab, slab_cells), :],
            tail.at[4], tail.at[5], device,
        )
    eta[pl.ds(slab_cells * place.slab, slab_cells), :] = cells[place.cell]

    acc[...] = jnp.zeros_like(acc)
    gram(acc, 0, True, block, block, depth, lambda t: t)

    @pl.loop(0, chunks)
    def _(k):
        await_bytes(
            work.at[:, :, pl.ds(0, step), pl.ds(0, rows * (slabs - 1)), :], sems.at[1, k]
        )

        @pl.loop(0, step)
        def _(i):
            z = k * step + i
            for comp in range(2):
                for ri in range(2):
                    work[comp, ri, z, pl.ds(rows * place.slab, rows), :] = block[
                        place.layer, comp, ri, half * place.core + z
                    ]
            across, along, planar = waves[0], waves[1], waves[2]
            deep = depths[half * place.core + z, 0:1, :]
            size = jnp.sqrt(planar * planar + deep * deep)
            fields = []
            for ri in range(2):
                one = work[0, ri, z]
                two = work[1, ri, z] * size
                upright = one * deep
                fields.append(
                    [across * upright - along * two, along * upright + across * two, -planar * one]
                )
            curled = jnp.concatenate(
                [jnp.concatenate([fields[0][c], fields[1][c]], 1) for c in range(3)], 0
            )
            lines = right_transform(curled, x_plus)
            stacked = jnp.concatenate(
                [
                    jnp.concatenate(
                        [
                            lines[c * height : (c + 1) * height, :width],
                            lines[c * height : (c + 1) * height, width:],
                        ],
                        0,
                    )
                    for c in range(3)
                ],
                1,
            )
            planes = left_transform(y_plus, stacked)
            for c in range(3):
                for ri in range(2):
                    for cell in range(2 * groups):
                        base = ri * height + cell * share
                        out_y[cell, c, ri, pl.ds(z * share, share), :] = planes[
                            base : base + share, c * width : (c + 1) * width
                        ]

        for i in range(1, 2 * groups):
            cell, device = place.plane_peer(i)
            send(
                out_y.at[cell, :, :, pl.ds(k * part, part), :],
                in_z.at[:, :, pl.ds(place.cell * half * share + k * part, part), :],
                sems.at[2, k], sems.at[3, k], device,
            )
        for c in range(3):
            for ri in range(2):
                in_z[c, ri, pl.ds(place.cell * half * share + k * part, part), :] = out_y[
                    place.cell, c, ri, pl.ds(k * part, part), :
                ]

    await_bytes(eta.at[pl.ds(0, slab_cells * (slabs - 1)), :], tail.at[5])

    @pl.loop(0, chunks)
    def _(k):
        await_bytes(in_z.at[:, :, pl.ds(0, part * (2 * groups - 1)), :], sems.at[3, k])

    @pl.loop(0, share // 2)
    def _(pair):
        weights = [eta[pl.ds(2 * pair + j, length, stride=share), :] for j in range(2)]
        for c in range(3):
            stacked = jnp.concatenate(
                [
                    jnp.concatenate(
                        [in_z[c, ri, pl.ds(2 * pair + j, length, stride=share), :] for ri in range(2)],
                        0,
                    )
                    for j in range(2)
                ],
                1,
            )
            field = left_transform(z_plus, stacked)
            weight = jnp.concatenate(weights, 1)
            field = field * jnp.concatenate([weight, weight], 0)
            back = left_transform(z_minus, field)
            for j in range(2):
                for ri in range(2):
                    out_z[c, ri, pl.ds(2 * pair + j, length, stride=share), :] = back[
                        ri * length : (ri + 1) * length, j * width : (j + 1) * width
                    ]

    @pl.loop(0, chunks)
    def _(k):
        for i in range(1, 2 * groups):
            cell, device = place.plane_peer(i)
            send(
                out_z.at[:, :, pl.ds(cell * half * share + k * part, part), :],
                in_y.at[place.cell, :, :, pl.ds(k * part, part), :],
                sems.at[4, k], sems.at[5, k], device,
            )

    @pl.loop(0, chunks)
    def _(k):
        for c in range(3):
            for ri in range(2):
                in_y[place.cell, c, ri, pl.ds(k * part, part), :] = out_z[
                    c, ri, pl.ds(place.cell * half * share + k * part, part), :
                ]
        await_bytes(
            in_y.at[pl.ds(0, 2 * groups - 1), :, :, pl.ds(0, part), :], sems.at[5, k]
        )

        @pl.loop(0, step)
        def _(i):
            z = k * step + i
            stacked = jnp.concatenate(
                [
                    jnp.concatenate(
                        [
                            in_y[cell, c, ri, pl.ds(z * share, share), :]
                            for ri in range(2)
                            for cell in range(2 * groups)
                        ],
                        0,
                    )
                    for c in range(3)
                ],
                1,
            )
            planes = left_transform(y_minus, stacked)
            lines = jnp.concatenate(
                [
                    jnp.concatenate(
                        [
                            planes[:height, c * width : (c + 1) * width],
                            planes[height:, c * width : (c + 1) * width],
                        ],
                        1,
                    )
                    for c in range(3)
                ],
                0,
            )
            curled = right_transform(lines, x_minus)
            across, along, planar = waves[0], waves[1], waves[2]
            deep = depths[half * place.core + z, 0:1, :]
            size = jnp.sqrt(planar * planar + deep * deep)
            for ri in range(2):
                fields = [
                    curled[c * height : (c + 1) * height, ri * width : (ri + 1) * width]
                    for c in range(3)
                ]
                work[0, ri, z] = deep * (across * fields[0] + along * fields[1]) - planar * fields[2]
                work[1, ri, z] = size * (across * fields[1] - along * fields[0])
            for comp in range(2):
                for ri in range(2):
                    image[place.layer, comp, ri, half * place.core + z] = work[
                        comp, ri, z, pl.ds(rows * place.slab, rows), :
                    ]

        for i in range(1, slabs):
            slab, device = place.slab_peer(i)
            send(
                work.at[:, :, pl.ds(k * step, step), pl.ds(rows * slab, rows), :],
                image.at[place.layer, :, :, pl.ds(half * place.core + k * step, step), :, :],
                sems.at[6, k], sems.at[7, k], device,
            )

    @pl.loop(0, chunks)
    def _(k):
        await_bytes(
            work.at[:, :, pl.ds(0, step), pl.ds(0, rows * (slabs - 1)), :], sems.at[7, k]
        )
        gram(
            acc, gram_rows(bands, True), True, block, image, 2 * step,
            lambda t: half * (t // step) + k * step + t % step,
        )

    sums[...] = total(place, mine, first, second, tail, lane_sums(tile, acc))

    @pl.loop(0, chunks)
    def _(k):
        slab_bytes = work.at[:, :, pl.ds(0, step), pl.ds(0, rows * (slabs - 1)), :]
        plane_bytes = in_z.at[:, :, pl.ds(0, part * (2 * groups - 1)), :]
        await_bytes(slab_bytes, sems.at[0, k])
        await_bytes(plane_bytes, sems.at[2, k])
        await_bytes(plane_bytes, sems.at[4, k])
        await_bytes(slab_bytes, sems.at[6, k])

    await_bytes(eta.at[pl.ds(0, slab_cells * (slabs - 1)), :], tail.at[4])


def second_kernel(
    groups, slabs, mixing, block, image, waves, depths, cells, x_plus, z_plus, y_plus,
    search, sums, out_x, in_z, out_z, in_y, eta, acc, field_acc, tile, mine, first, second,
    sems, tail,
):
    place = Place(groups, slabs)
    bands, _, _, depth, rows, width = block.shape
    length = depth * groups
    height = rows * slabs
    parts = rows // 8
    thin = length // slabs
    quarter = width // groups
    share = cells.shape[1] // thin

    enter(
        [place.slab_peer(i)[1] for i in range(1, slabs)]
        + [place.band_peer(i)[1] for i in range(1, groups)]
    )
    acc[...] = jnp.zeros_like(acc)
    field_acc[...] = jnp.zeros_like(field_acc)
    lane = lax.broadcasted_iota(jnp.int32, (1, width), 1) // quarter
    deep_step = 8 if depth % 8 == 0 else 1

    @pl.loop(0, parts)
    def _(part):
        band_rows = pl.ds(part * 8, 8)
        across, along, planar = (waves[place.slab, i, band_rows, :] for i in range(3))

        @pl.loop(0, depth)
        def _(z):
            tile_at = (z, band_rows, slice(None))
            deep = depths[z]
            scale = 1.0 / (planar * planar + deep * deep + 1.0)
            for comp in range(2):
                reals = [block[(i, comp, 0) + tile_at] for i in range(bands)]
                imags = [block[(i, comp, 1) + tile_at] for i in range(bands)]
                for j in range(bands):
                    real = image[(j, comp, 0) + tile_at]
                    imag = image[(j, comp, 1) + tile_at]
                    for i in range(bands):
                        real = real - (reals[i] * mixing[i, j] - imags[i] * mixing[bands + i, j])
                        imag = imag - (reals[i] * mixing[bands + i, j] + imags[i] * mixing[i, j])
                    search[(j, comp, 0) + tile_at] = real * scale
                    search[(j, comp, 1) + tile_at] = imag * scale

        @pl.loop(0, depth // deep_step)
        def _(group):
            planes = pl.ds(group * deep_step, deep_step)
            deep = depths[planes]
            size = jnp.sqrt(planar * planar + deep * deep)
            count = deep_step * 8
            lines = []
            for i in range(bands):
                fields = []
                for ri in range(2):
                    one = search[i, 0, ri, planes, band_rows, :]
                    two = search[i, 1, ri, planes, band_rows, :] * size
                    upright = one * deep
                    fields.append(
                        [
                            value.reshape(count, width)
                            for value in (
                                across * upright - along * two,
                                along * upright + across * two,
                                -planar * one,
                            )
                        ]
                    )
                curled = jnp.concatenate(
                    [jnp.concatenate([fields[0][c], fields[1][c]], 1) for c in range(3)], 0
                )
                lines.append(right_transform(curled, x_plus.at[i]))
            at = pl.ds(group * count, count)
            for target in range(groups):
                for ri in range(2):
                    columns = slice(ri * width, (ri + 1) * width)
                    packed = lines[(-target) % groups][:, columns]
                    for spot in range(1, groups):
                        packed = jnp.where(
                            lane == spot, lines[(spot - target) % groups][:, columns], packed
                        )
                    for c in range(3):
                        out_x[part, target, c, ri, at, :] = packed[c * count : (c + 1) * count]

        for c in range(3):
            for i in range(1, groups):
                group, device = place.band_peer(i)
                send(
                    out_x.at[part, group, c],
                    in_z.at[part, c, :, pl.ds(depth * 8 * place.group, depth * 8), :],
                    sems.at[0, part * 3 + c], sems.at[1, part * 3 + c], device,
                )
            for ri in range(2):
                in_z[part, c, ri, pl.ds(depth * 8 * place.group, depth * 8), :] = out_x[
                    part, place.group, c, ri
                ]

    @pl.loop(0, 3 * parts)
    def _(k):
        part, c = k // 3, k % 3
        await_bytes(in_z.at[part, c, :, pl.ds(0, depth * 8 * (groups - 1)), :], sems.at[1, k])

        @pl.loop(0, 4)
        def _(pair):
            stacked = jnp.concatenate(
                [
                    jnp.concatenate(
                        [
                            in_z[part, c, ri, pl.ds(2 * pair + j, length, stride=8), :]
                            for ri in range(2)
                        ],
                        0,
                    )
                    for j in range(2)
                ],
                1,
            )
            columns = left_transform(z_plus, stacked)
            for j in range(2):
                for ri in range(2):
                    out_z[part, c, ri, pl.ds(2 * pair + j, length, stride=8), :] = columns[
                        ri * length : (ri + 1) * length, j * width : (j + 1) * width
                    ]

        for i in range(1, slabs):
            slab, device = place.slab_peer(i)
            send(
                out_z.at[part, c, :, pl.ds(thin * 8 * slab, thin * 8), :],
                in_y.at[c, place.slab, part],
                sems.at[2, k], sems.at[3, k], device,
            )
        for ri in range(2):
            in_y[c, place.slab, part, ri] = out_z[
                part, c, ri, pl.ds(thin * 8 * place.slab, thin * 8), :
            ]

    @pl.loop(0, thin)
    def _(z):
        for cell in range(2 * groups):
            values = cells[cell, pl.ds(z * share, share), :]
            values = pltpu.roll(values, lax.rem(width - quarter * place.group, width), 1)
            values = jnp.where(lane == 0, values, 0.0)
            reach = quarter
            while reach < width:
                values = values + pltpu.roll(values, reach, 1)
                reach *= 2
            eta[z, cell * share : (cell + 1) * share, :] = values

    base = gram(acc, 0, False, block, search, depth, lambda t: t)
    base = gram(acc, base, True, search, search, depth, lambda t: t)
    gram(acc, base, False, search, image, depth, lambda t: t)

    for c in range(3):
        for part in range(parts):
            await_bytes(
                in_y.at[c, pl.ds(0, slabs - 1), part], sems.at[3, part * 3 + c]
            )

        @pl.loop(0, thin)
        def _(z, c=c):
            stacked = jnp.concatenate(
                [
                    in_y[c, slab, part, ri, pl.ds(8 * z, 8), :]
                    for ri in range(2)
                    for slab in range(slabs)
                    for part in range(parts)
                ],
                0,
            )
            field = left_transform(y_plus, stacked)
            real, imag = field[:height], field[height:]
            weight = eta[z]
            real_weighted, imag_weighted = real * weight, imag * weight
            for shift in range(bands // 2 + 1):
                if shift == 0:
                    real_other, imag_other = real, imag
                else:
                    real_other = pltpu.roll(real, quarter * shift, 1)
                    imag_other = pltpu.roll(imag, quarter * shift, 1)
                real_term = real_weighted * real_other + imag_weighted * imag_other
                imag_term = real_weighted * imag_other - imag_weighted * real_other
                for place_of, term in ((2 * shift, real_term), (2 * shift + 1, imag_term)):
                    field_acc[place_of] += jnp.sum(term.reshape(height // 8, 8, width), axis=0)

    pieces = jnp.sum(field_acc[...], axis=1)
    pieces = pltpu.roll(pieces, lax.rem(width - quarter * place.group, width), 1)
    values = lane_sums(tile, acc)
    message = jnp.concatenate([values, jnp.zeros((pieces.shape[0], values.shape[1]), jnp.float32)], 0)
    if values.shape[1] > width:
        pieces = jnp.concatenate(
            [pieces, jnp.zeros((pieces.shape[0], values.shape[1] - width), jnp.float32)], 1
        )
    message = jnp.concatenate([values, pieces], 0)
    sums[...] = total(place, mine, first, second, tail, message)

    @pl.loop(0, 3 * parts)
    def _(k):
        await_bytes(in_z.at[0, 0, :, pl.ds(0, depth * 8 * (groups - 1)), :], sems.at[0, k])
        await_bytes(in_y.at[0, pl.ds(0, slabs - 1), 0], sems.at[2, k])


def vmem(count):
    return [pl.BlockSpec(memory_space=pltpu.VMEM)] * count


def round_up(value, step):
    return -(-value // step) * step


def first_operator(block, waves, depths, cells, groups, slabs):
    bands, _, _, depth, rows, width = block.shape
    half, height, length = depth // 2, rows * slabs, depth * groups
    share = height // (2 * groups)
    count = 2 * gram_rows(bands, True)
    lanes = round_up(count, width)
    chunks = half // step_count(half)
    single = lambda *shape: pltpu.VMEM(shape, jnp.float32)
    tables = [
        jnp.asarray(right_table(dft_matrix(width, 1.0).T)),
        jnp.asarray(left_table(height, 1.0)),
        jnp.asarray(left_table(length, 1.0)),
        jnp.asarray(left_table(length, -1.0)),
        jnp.asarray(left_table(height, -1.0)),
        jnp.asarray(right_table(dft_matrix(width, -1.0).T)),
    ]
    return pl.pallas_call(
        partial(first_kernel, groups, slabs),
        in_specs=vmem(4 + len(tables)),
        out_specs=vmem(2),
        out_shape=[
            jax.ShapeDtypeStruct(block.shape, jnp.float32),
            jax.ShapeDtypeStruct((8, lanes), jnp.float32),
        ],
        scratch_shapes=[
            single(2, 2, half, height, width),
            single(2 * groups, 3, 2, half * share, width),
            single(3, 2, length * share, width),
            single(3, 2, length * share, width),
            single(2 * groups, 3, 2, half * share, width),
            single(length * share, width),
            single(count, 8, width),
            single(lanes, width),
            single(2, 8, lanes),
            single(slabs, 8, lanes),
            single(groups, 8, lanes),
            pltpu.SemaphoreType.DMA((8, chunks)),
            pltpu.SemaphoreType.DMA((6,)),
        ],
        compiler_params=pltpu.CompilerParams(
            collective_id=0, has_side_effects=True, vmem_limit_bytes=VMEM_LIMIT
        ),
    )(block, waves, depths, cells, *tables)


def second_operator(mixing, block, image, waves, depths, cells, groups, slabs):
    bands, _, _, depth, rows, width = block.shape
    height, length = rows * slabs, depth * groups
    thin, parts, quarter = length // slabs, rows // 8, width // groups
    count = 2 * gram_rows(bands, False) + gram_rows(bands, True)
    lanes = round_up(count, width)
    field_rows = round_up(2 * (bands // 2 + 1), 8)
    message = (8 + field_rows, lanes)
    single = lambda *shape: pltpu.VMEM(shape, jnp.float32)
    plain = dft_matrix(width, 1.0).T
    orders = []
    for band in range(bands):
        spots = np.arange(width) // quarter
        source = ((spots - band) % groups) * quarter + np.arange(width) % quarter
        orders.append(right_table(plain[:, np.concatenate([source, width + source])]))
    tables = [
        jnp.asarray(np.stack(orders)),
        jnp.asarray(left_table(length, 1.0)),
        jnp.asarray(left_table(height, 1.0)),
    ]
    return pl.pallas_call(
        partial(second_kernel, groups, slabs),
        in_specs=[pl.BlockSpec(memory_space=pltpu.SMEM)] + vmem(5 + len(tables)),
        out_specs=vmem(2),
        out_shape=[
            jax.ShapeDtypeStruct(block.shape, jnp.float32),
            jax.ShapeDtypeStruct(message, jnp.float32),
        ],
        scratch_shapes=[
            single(parts, groups, 3, 2, depth * 8, width),
            single(parts, 3, 2, length * 8, width),
            single(parts, 3, 2, length * 8, width),
            single(3, slabs, parts, 2, thin * 8, width),
            single(thin, height, width),
            single(count, 8, width),
            single(field_rows, 8, width),
            single(lanes, width),
            single(2, *message),
            single(slabs, *message),
            single(groups, *message),
            pltpu.SemaphoreType.DMA((4, 3 * parts)),
            pltpu.SemaphoreType.DMA((4,)),
        ],
        compiler_params=pltpu.CompilerParams(
            collective_id=1, has_side_effects=True, vmem_limit_bytes=VMEM_LIMIT
        ),
    )(mixing, block, image, waves, depths, cells, *tables)


def shards(band_block, material_grid, inverse_permittivity, bloch_index):
    groups, slabs = lax.axis_size("band"), lax.axis_size("slab")
    bands, _, _, depth, rows, width = band_block.shape
    length, height = depth * groups, rows * slabs
    grid_cells = length * height * width
    thin = length // slabs
    share = height // (2 * groups)
    fraction = (bloch_index[0].astype(jnp.float32) + 1.0) / KPOINTS
    width_wave = axis_values(width, 0.5, fraction, 0, width)[None, :]
    height_wave = axis_values(height, 0.35, fraction, 0, height)[:, None]
    planar = jnp.sqrt(width_wave * width_wave + height_wave * height_wave)
    waves = jnp.stack([width_wave / planar, height_wave / planar, planar])
    depth_wave = axis_values(length, 0.2, fraction, lax.axis_index("band") * depth, depth)
    depths = jnp.broadcast_to(depth_wave[:, None, None], (depth, 8, width))
    grouped = material_grid.reshape(thin, 2 * groups, share, width).transpose(1, 0, 2, 3)
    grouped = grouped.reshape(2 * groups, thin * share, width)
    cells = jnp.zeros(grouped.shape, jnp.float32)
    for material in range(inverse_permittivity.shape[0]):
        cells = jnp.where(grouped == material, inverse_permittivity[material] / grid_cells, cells)

    image, sums = first_operator(band_block, waves, depths, cells, groups, slabs)
    size = gram_rows(bands, True)
    flat = sums[0] / grid_cells
    own_real, own_imag = unpack(flat[:size], bands, True)
    cross_real, cross_imag = unpack(flat[size : 2 * size], bands, True)
    join = lambda rows: jnp.concatenate([jnp.concatenate(row, 1) for row in rows], 0)
    system = join([[own_real, -own_imag], [own_imag, own_real]])
    right_side = jnp.concatenate([cross_real, cross_imag], 0)
    factor = jnp.linalg.cholesky(system)
    mixing = jax.scipy.linalg.cho_solve((factor, True), right_side)

    by_slab = waves.reshape(3, slabs, rows, width).transpose(1, 0, 2, 3)
    search_block, sums = second_operator(
        mixing, band_block, image, by_slab, depths, cells, groups, slabs
    )
    sums = sums / grid_cells
    size = 2 * bands * bands
    flat = sums[0]
    mixed_real, mixed_imag = unpack(flat[:size], bands, False)
    search_real, search_imag = unpack(flat[size : size + gram_rows(bands, True)], bands, True)
    flat = flat[size + gram_rows(bands, True) :]
    back_real, back_imag = unpack(flat[:size], bands, False)
    field = sums[8:, :width].reshape(-1, groups, width // groups).sum(2)
    real = [[None] * bands for _ in range(bands)]
    imag = [[None] * bands for _ in range(bands)]
    for i in range(bands):
        for shift in range(bands // 2 + 1):
            j = (i - shift) % bands
            real[i][j], imag[i][j] = field[2 * shift, i], field[2 * shift + 1, i]
            real[j][i], imag[j][i] = real[i][j], -imag[i][j]
    stack = lambda rows: jnp.stack([jnp.stack(row) for row in rows])
    field_real, field_imag = stack(real), stack(imag)
    correlation = jnp.stack(
        [
            join([[own_real, mixed_real], [mixed_real.T, search_real]]),
            join([[own_imag, mixed_imag], [-mixed_imag.T, search_imag]]),
        ]
    )
    projected = jnp.stack(
        [
            join([[cross_real, back_real.T], [back_real, field_real]]),
            join([[cross_imag, -back_imag.T], [back_imag, field_imag]]),
        ]
    )
    return (search_block, correlation, projected)


def solution(mesh):
    return jax.shard_map(
        shards,
        mesh=mesh,
        in_specs=(P(None, None, None, "band", "slab", None), P("slab", None, None), P(), P()),
        out_specs=(P(None, None, None, "band", "slab", None), P(), P()),
        check_vma=False,
    )
```

time: 1090 us -> 587 us (0.54); the launches traced: 1080 us -> 585 us
  blocking collectives: 520 us -> 0 us
  Pallas kernels: 38.9 us -> 429 us
  waiting for transfers between devices: 248 us -> 0 us
  matrix products: 157 us -> 0.94 us
  other arithmetic: 32.5 us -> 116 us
  local copies, waits for them, and re-layouts: 54 us -> 17.1 us
  starting transfers between devices: 20.4 us -> 0 us
  between operations: 4.88 us -> 21.8 us
    all_to_all x4 -> x0, blocking collectives: 474 us -> none  [the longest x2 283 us: slab_operator(): lax.all_to_all(transform(spatial, 3, -1.0), 'slab', split_axis=3, concat_...]
    pallas_call x5 -> x2, Pallas kernels: 38.9 us -> 429 us  [the longest x1 254 us: first_operator(): pl.pallas_call(partial(first_kernel, groups, slabs), in_specs=vmem(4 + le...]
    all_to_all x4 -> x0, waiting for transfers between devices: 248 us -> none  [the longest x1 133 us: slab_operator(): lax.all_to_all(spectrum, 'slab', split_axis=2, concat_axis=3, tiled=True)]
    dot_general x48 -> x0, matrix products: 156 us -> none  [the longest x24 77.9 us: transform(): new_real = contract(real_part, cosine) - contract(imaginary, sine_table)]
    another operation x14 -> x57, other arithmetic: 5.92 us -> 110 us  [the longest x42 92.3 us: unpack(): stack = lambda rows: jnp.stack([jnp.stack(row) for row in rows])]
    unnamed x4 -> x0, blocking collectives: 46.6 us -> none
    another operation x8 -> x18, local copies, waits for them, and re-layouts: 26.3 us -> 1.66 us  [unpack(): stack = lambda rows: jnp.stack([jnp.stack(row) for row in rows])]
    all_to_all x4 -> x0, starting transfers between devices: 20.4 us -> none  [the longest x2 9.82 us: slab_operator(): lax.all_to_all(local_image, 'band', split_axis=3, concat_axis=0, tiled=True)]
  transfers between devices with their start and end apart: 4 -> 0, of which waited for: 4 -> 0; matrix products, arithmetic and copies ran while one was open for 1% -> 0% of each run, Pallas kernels for 2% -> 0%
where the time goes in v1:
time: 587 us; the launch traced here: 585 us
  Pallas kernels  429 us (73%)
  other arithmetic  116 us (20%)
  between operations  21.8 us (4%)
  local copies, waits for them, and re-layouts  17.1 us (3%)
    pallas_call x1, Pallas kernels, first_operator(): pl.pallas_call(partial(first_kernel, groups, slabs), in_specs=vmem(4 + le...  254 us
    pallas_call x1, Pallas kernels, second_operator(): pl.pallas_call(partial(second_kernel, groups, slabs), in_specs=[pl.BlockS...  175 us
    another operation x42, other arithmetic, unpack(): stack = lambda rows: jnp.stack([jnp.stack(row) for row in rows])  92.3 us
    another operation x8, other arithmetic, shards(): stack = lambda rows: jnp.stack([jnp.stack(row) for row in rows])  14.5 us

profile of v1, /device:TPU:0, one launch (start us, length us, event | category | flops | bytes accessed | tf_op | source)
XLA Modules:
  0.0 584.5 jit_solution(5923180837101840800)
XLA Ops:
  10.3 253.9 %shard_map.148 = (f32[4,2,2,32,16,128]{5,4,3,2,1,0:T(8,128)}, f32[8,128]{1,0:T(8,128)}) custom-call(f32[4,2,2,32,16,128]{5,4,3,2,1,0:T(8,128)} %block.3, f32[3,128,128]{2,1,0:T(8,128)} %pad_maximum_fusion.waves, f32[32,8,128]{2,1,0:T(8,128)} %broadcast_in_dim.26.depths, f32[8,256,128]{2,1,0:T(8,128)} %bitcast.294, bf16[768,256]{1,0:T(8,128)(2,1)} %constant.126.clone.x_plus, ...), custom_call_target="tpu_custom_call" | custom-call | tf_op jit(solution)/shard_map/pallas_call | solution.py:663
  273.9 2.6 maximum_bitcast_fusion.16
  279.1 2.6 maximum_bitcast_fusion.14
  286.3 2.6 maximum_bitcast_fusion.8
  290.9 2.6 maximum_bitcast_fusion.13
  293.5 2.6 maximum_bitcast_fusion.12
  298.2 2.6 maximum_bitcast_fusion.4
  303.3 2.7 maximum_bitcast_fusion.6
  313.2 174.9 %shard_map.149 = (f32[4,2,2,32,16,128]{5,4,3,2,1,0:T(8,128)}, f32[16,128]{1,0:T(8,128)}) custom-call(f32[8,4]{1,0:T(8,128)} %fusion.12.mixing, f32[4,2,2,32,16,128]{5,4,3,2,1,0:T(8,128)} %block.3, f32[4,2,2,32,16,128]{5,4,3,2,1,0:T(8,128)} %get-tuple-element.8.image, f32[8,3,16,128]{3,2,1,0:T(8,128)} %maximum_bitcast_fusion.waves, ...), custom_call_target="tpu_custom_call" | custom-call | tf_op jit(solution)/shard_map/pallas_call | solution.py:712
  489.4 2.7 maximum_bitcast_fusion.21
  494.8 2.6 maximum_bitcast_fusion.38
  500.6 2.6 maximum_bitcast_fusion.36
  503.2 2.6 maximum_bitcast_fusion.39
  505.8 2.6 maximum_bitcast_fusion.47
  513.4 2.6 maximum_bitcast_fusion.44
  517.0 2.7 maximum_bitcast_fusion.22
  519.7 2.7 maximum_bitcast_fusion.27
  535.6 2.6 maximum_bitcast_fusion.20
  542.2 2.6 maximum_bitcast_fusion.28
  544.8 2.7 maximum_bitcast_fusion.32
  547.5 2.6 maximum_bitcast_fusion.31
  568.9 2.7 maximum_bitcast_fusion.40
  574.1 2.6 maximum_bitcast_fusion.42
  579.9 4.6 copy.45
  (98 shorter events, 74.1 us)

commit v2 on v1

--- a/solution.py
+++ b/solution.py
@@ -13,12 +13,6 @@
 HIGHEST = lax.Precision.HIGHEST
 MESH = pl.DeviceIdType.MESH
 VMEM_LIMIT = 60 * 1024 * 1024
-
-
-def axis_values(length, weight, fraction, offset, extent):
-    indices = offset + jnp.arange(extent, dtype=jnp.int32)
-    signed = jnp.where(indices >= length // 2, indices - length, indices).astype(jnp.float32)
-    return 2.0 * math.pi / length * (signed + weight * fraction)
 
 
 def halves(values):
@@ -102,18 +96,134 @@
     return bands * (bands + 1) if hermitian else 2 * bands * bands
 
 
-def unpack(flat, bands, hermitian):
-    real = [[None] * bands for _ in range(bands)]
-    imag = [[None] * bands for _ in range(bands)]
-    place = 0
-    for i in range(bands):
-        for j in range(i if hermitian else 0, bands):
-            real[i][j], imag[i][j] = flat[place], flat[place + 1]
-            if hermitian and j > i:
-                real[j][i], imag[j][i] = flat[place], -flat[place + 1]
-            place += 2
-    stack = lambda rows: jnp.stack([jnp.stack(row) for row in rows])
-    return stack(real), stack(imag)
+def scatter_tables(entries, pieces, width):
+    slots = {}
+    rows = 8 * (-(-(1 + max(entry[2] for entry in entries)) // 8))
+    for source, lane, row, column, sign in entries:
+        columns = slots.setdefault((source, lane), {})
+        columns.setdefault(column, {})[row] = sign
+    blocks = []
+    for source in range(pieces):
+        depth = max([len(v) for (s, _), v in slots.items() if s == source], default=0)
+        blocks += [(source, place) for place in range(depth)]
+    spread = np.zeros((rows, width * len(blocks)), np.float32)
+    gather = np.zeros((width * len(blocks), width), np.float32)
+    for index, (source, place) in enumerate(blocks):
+        for lane in range(width):
+            columns = list(slots.get((source, lane), {}).items())
+            if place < len(columns):
+                column, signs = columns[place]
+                gather[index * width + lane, column] = 1.0
+                for row, sign in signs.items():
+                    spread[row, index * width + lane] = sign
+    return [source for source, _ in blocks], spread, gather.astype(jnp.bfloat16)
+
+
+def scatter(values, sources, spread, gather):
+    rows, width = spread.shape[0], values[0].shape[1]
+    spots = jnp.concatenate(
+        [
+            jnp.broadcast_to(values[source], (rows, width))
+            * spread[:, place * width : (place + 1) * width]
+            for place, source in enumerate(sources)
+        ],
+        1,
+    )
+    high, rest = halves(spots)
+    low = (spots - high.astype(jnp.float32)) - rest.astype(jnp.float32)
+    return (dot(high, gather[...]) + dot(rest, gather[...])) + dot(
+        low.astype(jnp.bfloat16), gather[...]
+    )
+
+
+def pair_list(bands, hermitian):
+    return [(i, j) for i in range(bands) for j in range(i if hermitian else 0, bands)]
+
+
+def complex_entries(source, base, pairs, put):
+    entries = []
+    for place, (i, j) in enumerate(pairs):
+        for real_row, imag_row, column, sign in put(i, j):
+            lane = base + 2 * place
+            entries.append((source + lane // 128, lane % 128, real_row, column, 1.0))
+            entries.append((source + (lane + 1) // 128, (lane + 1) % 128, imag_row, column, sign))
+    return entries
+
+
+def mirrored(i, j, put):
+    return [put(i, j, 1.0)] if i == j else [put(i, j, 1.0), put(j, i, -1.0)]
+
+
+def system_entries(bands):
+    pairs = pair_list(bands, True)
+    entries = []
+    for offset in (0, bands):
+        def left(i, j, sign):
+            if offset == 0:
+                return (i, bands + i, j, sign)
+            return (bands + i, i, bands + j, -sign)
+
+        entries += complex_entries(0, 0, pairs, lambda i, j: mirrored(i, j, left))
+    right = lambda i, j, sign: (i, bands + i, 2 * bands + j, sign)
+    return entries + complex_entries(
+        0, gram_rows(bands, True), pairs, lambda i, j: mirrored(i, j, right)
+    )
+
+
+def result_entries(bands, width, first_pieces, second_pieces):
+    size, own = 2 * bands, pair_list(bands, True)
+    every = pair_list(bands, False)
+
+    def spot(matrix, row, column):
+        return lambda i, j, sign: (
+            2 * size * matrix + row + i, 2 * size * matrix + size + row + i, column + j, sign
+        )
+
+    entries = complex_entries(0, 0, own, lambda i, j: mirrored(i, j, spot(0, 0, 0)))
+    entries += complex_entries(
+        0, gram_rows(bands, True), own, lambda i, j: mirrored(i, j, spot(1, 0, 0))
+    )
+    source, base = first_pieces, 0
+    entries += complex_entries(
+        source, base, every,
+        lambda i, j: [spot(0, 0, bands)(i, j, 1.0), spot(0, bands, 0)(j, i, -1.0)],
+    )
+    base += gram_rows(bands, False)
+    entries += complex_entries(
+        source, base, own, lambda i, j: mirrored(i, j, spot(0, bands, bands))
+    )
+    base += gram_rows(bands, True)
+    entries += complex_entries(
+        source, base, every,
+        lambda i, j: [spot(1, bands, 0)(i, j, 1.0), spot(1, 0, bands)(j, i, -1.0)],
+    )
+    source += second_pieces
+    for shift in range(bands // 2 + 1):
+        for lane in range(width):
+            i = lane // (width // bands)
+            j = (i - shift) % bands
+            places = [(i, j, 1.0)]
+            if shift and 2 * shift != bands:
+                places.append((j, i, -1.0))
+            for row, column, sign in places:
+                real_row, imag_row, at, sign = spot(1, bands, bands)(row, column, sign)
+                entries.append((source + 2 * shift, lane, real_row, at, 1.0))
+                if shift:
+                    entries.append((source + 2 * shift + 1, lane, imag_row, at, sign))
+    return entries
+
+
+def solve(system, size, width):
+    row_at = lax.broadcasted_iota(jnp.int32, system.shape, 0)
+    for k in range(size):
+        pivot = system[k : k + 1, :] / system[k : k + 1, k : k + 1]
+        system = jnp.where(row_at == k, pivot, system - system[:, k : k + 1] * pivot)
+    return system
+
+
+def wave(length, weight, fraction, indices):
+    signed = jnp.where(indices >= length // 2, indices - length, indices).astype(jnp.float32)
+    return 2.0 * math.pi / length * (signed + weight * fraction)
 
 
 class Place:
@@ -194,9 +304,15 @@
     )
 
 
-def first_kernel(
-    groups, slabs, block, waves, depths, cells, x_plus, y_plus, z_plus, z_minus, y_minus, x_minus,
-    image, sums, work, out_y, in_z, out_z, in_y, eta, acc, tile, mine, first, second, sems, tail,
+def step_kernel(
+    groups, slabs, solve_sources, result_sources,
+    permittivity, bloch, block, materials, x_plus, x_split, x_minus, y_plus, y_minus, z_plus,
+    z_minus, solve_spread, solve_gather, result_spread, result_gather,
+    search, results,
+    work, image, out_y, in_z, out_z, in_y, out_x, eta, local_eta, cells, waves, depths, mixing,
+    first_acc, first_tile, first_mine, first_slab, first_band,
+    second_acc, field_acc, second_tile, second_mine, second_slab, second_band,
+    sems, ends, tail,
 ):
     place = Place(groups, slabs)
     bands, _, _, depth, rows, width = block.shape
@@ -204,6 +320,7 @@
     height = rows * slabs
     length = depth * groups
     share = out_y.shape[3] // half
+    cell_count = length * height * width
     step = step_count(half)
     chunks = half // step
     part = step * share
@@ -227,18 +344,39 @@
                 sems.at[0, k], sems.at[1, k], device,
             )
 
+    @pl.loop(0, length // slabs)
+    def _(z):
+        for cell in range(2 * groups):
+            found = materials[z, cell * share : (cell + 1) * share, :]
+            values = jnp.zeros(found.shape, jnp.float32)
+            for material in range(permittivity.shape[0]):
+                values = jnp.where(found == material, permittivity[material] / cell_count, values)
+            cells[cell, pl.ds(z * share, share), :] = values
+
     slab_cells = cells.shape[1]
     for i in range(1, slabs):
         slab, device = place.slab_peer(i)
         send(
             cells.at[2 * place.group + slab % 2],
             eta.at[pl.ds(slab_cells * place.slab, slab_cells), :],
-            tail.at[4], tail.at[5], device,
+            tail.at[2, 0], tail.at[2, 1], device,
         )
     eta[pl.ds(slab_cells * place.slab, slab_cells), :] = cells[place.cell]
 
-    acc[...] = jnp.zeros_like(acc)
-    gram(acc, 0, True, block, block, depth, lambda t: t)
+    fraction = (bloch[0].astype(jnp.float32) + 1.0) / KPOINTS
+    at_x = lax.broadcasted_iota(jnp.int32, (height, width), 1)
+    at_y = lax.broadcasted_iota(jnp.int32, (height, width), 0)
+    wave_x, wave_y = wave(width, 0.5, fraction, at_x), wave(height, 0.35, fraction, at_y)
+    planar = jnp.sqrt(wave_x * wave_x + wave_y * wave_y)
+    waves[0], waves[1], waves[2] = wave_x / planar, wave_y / planar, planar
+
+    @pl.loop(0, depth)
+    def _(z):
+        at_z = jnp.broadcast_to(place.group * depth + z, (8, width))
+        depths[z] = wave(length, 0.2, fraction, at_z)
+
+    first_acc[...] = jnp.zeros_like(first_acc)
+    gram(first_acc, 0, True, block, block, depth, lambda t: t)
 
     @pl.loop(0, chunks)
     def _(k):
@@ -304,7 +442,7 @@
                     place.cell, c, ri, pl.ds(k * part, part), :
                 ]
 
-    await_bytes(eta.at[pl.ds(0, slab_cells * (slabs - 1)), :], tail.at[5])
+    await_bytes(eta.at[pl.ds(0, slab_cells * (slabs - 1)), :], tail.at[2, 1])
 
     @pl.loop(0, chunks)
     def _(k):
@@ -417,11 +555,22 @@
             work.at[:, :, pl.ds(0, step), pl.ds(0, rows * (slabs - 1)), :], sems.at[7, k]
         )
         gram(
-            acc, gram_rows(bands, True), True, block, image, 2 * step,
+            first_acc, gram_rows(bands, True), True, block, image, 2 * step,
             lambda t: half * (t // step) + k * step + t % step,
         )
 
-    sums[...] = total(place, mine, first, second, tail, lane_sums(tile, acc))
+    first_sums = total(place, first_mine, first_slab, first_band, tail.at[0], lane_sums(first_tile, first_acc))
+    pieces = lambda values, row: [
+        values[row : row + 1, at : at + width] for at in range(0, values.shape[1], width)
+    ]
+    system = solve(
+        scatter(pieces(first_sums, 0), solve_sources, solve_spread, solve_gather), 2 * bands, width
+    )
+    for row in range(2 * bands):
+        for j in range(bands):
+            mixing[row, j] = jnp.broadcast_to(
+                system[row : row + 1, 2 * bands + j : 2 * bands + j + 1], (8, width)
+            )
 
     @pl.loop(0, chunks)
     def _(k):
@@ -432,28 +581,12 @@
         await_bytes(plane_bytes, sems.at[4, k])
         await_bytes(slab_bytes, sems.at[6, k])
 
-    await_bytes(eta.at[pl.ds(0, slab_cells * (slabs - 1)), :], tail.at[4])
-
-
-def second_kernel(
-    groups, slabs, mixing, block, image, waves, depths, cells, x_plus, z_plus, y_plus,
-    search, sums, out_x, in_z, out_z, in_y, eta, acc, field_acc, tile, mine, first, second,
-    sems, tail,
-):
-    place = Place(groups, slabs)
-    bands, _, _, depth, rows, width = block.shape
-    length = depth * groups
-    height = rows * slabs
+    await_bytes(eta.at[pl.ds(0, slab_cells * (slabs - 1)), :], tail.at[2, 0])
+
     parts = rows // 8
     thin = length // slabs
     quarter = width // groups
-    share = cells.shape[1] // thin
-
-    enter(
-        [place.slab_peer(i)[1] for i in range(1, slabs)]
-        + [place.band_peer(i)[1] for i in range(1, groups)]
-    )
-    acc[...] = jnp.zeros_like(acc)
+    second_acc[...] = jnp.zeros_like(second_acc)
     field_acc[...] = jnp.zeros_like(field_acc)
     lane = lax.broadcasted_iota(jnp.int32, (1, width), 1) // quarter
     deep_step = 8 if depth % 8 == 0 else 1
@@ -461,7 +594,9 @@
     @pl.loop(0, parts)
     def _(part):
         band_rows = pl.ds(part * 8, 8)
-        across, along, planar = (waves[place.slab, i, band_rows, :] for i in range(3))
+        across, along, planar = (
+            waves[i, pl.ds(rows * place.slab + part * 8, 8), :] for i in range(3)
+        )
 
         @pl.loop(0, depth)
         def _(z):
@@ -506,7 +641,7 @@
                 curled = jnp.concatenate(
                     [jnp.concatenate([fields[0][c], fields[1][c]], 1) for c in range(3)], 0
                 )
-                lines.append(right_transform(curled, x_plus.at[i]))
+                lines.append(right_transform(curled, x_split.at[i]))
             at = pl.ds(group * count, count)
             for target in range(groups):
                 for ri in range(2):
@@ -517,25 +652,26 @@
                             lane == spot, lines[(spot - target) % groups][:, columns], packed
                         )
                     for c in range(3):
-                        out_x[part, target, c, ri, at, :] = packed[c * count : (c + 1) * count]
+                        out_x[part * groups + target, c, ri, at, :] = packed[c * count : (c + 1) * count]
 
         for c in range(3):
             for i in range(1, groups):
                 group, device = place.band_peer(i)
                 send(
-                    out_x.at[part, group, c],
-                    in_z.at[part, c, :, pl.ds(depth * 8 * place.group, depth * 8), :],
-                    sems.at[0, part * 3 + c], sems.at[1, part * 3 + c], device,
+                    out_x.at[part * groups + group, c],
+                    in_z.at[c, :, pl.ds((part * length + depth * place.group) * 8, depth * 8), :],
+                    ends.at[0, part * 3 + c], ends.at[1, part * 3 + c], device,
                 )
             for ri in range(2):
-                in_z[part, c, ri, pl.ds(depth * 8 * place.group, depth * 8), :] = out_x[
-                    part, place.group, c, ri
+                in_z[c, ri, pl.ds((part * length + depth * place.group) * 8, depth * 8), :] = out_x[
+                    part * groups + place.group, c, ri
                 ]
 
     @pl.loop(0, 3 * parts)
     def _(k):
         part, c = k // 3, k % 3
-        await_bytes(in_z.at[part, c, :, pl.ds(0, depth * 8 * (groups - 1)), :], sems.at[1, k])
+        await_bytes(in_z.at[c, :, pl.ds(0, depth * 8 * (groups - 1)), :], ends.at[1, k])
+        base = part * length * 8
 
         @pl.loop(0, 4)
         def _(pair):
@@ -543,7 +679,7 @@
                 [
                     jnp.concatenate(
                         [
-                            in_z[part, c, ri, pl.ds(2 * pair + j, length, stride=8), :]
+                            in_z[c, ri, pl.ds(base + 2 * pair + j, length, stride=8), :]
                             for ri in range(2)
                         ],
                         0,
@@ -555,20 +691,20 @@
             columns = left_transform(z_plus, stacked)
             for j in range(2):
                 for ri in range(2):
-                    out_z[part, c, ri, pl.ds(2 * pair + j, length, stride=8), :] = columns[
+                    out_z[c, ri, pl.ds(base + 2 * pair + j, length, stride=8), :] = columns[
                         ri * length : (ri + 1) * length, j * width : (j + 1) * width
                     ]
 
         for i in range(1, slabs):
             slab, device = place.slab_peer(i)
             send(
-                out_z.at[part, c, :, pl.ds(thin * 8 * slab, thin * 8), :],
-                in_y.at[c, place.slab, part],
-                sems.at[2, k], sems.at[3, k], device,
+                out_z.at[c, :, pl.ds(base + thin * 8 * slab, thin * 8), :],
+                in_y.at[place.slab, c, :, pl.ds(part * thin * 8, thin * 8), :],
+                ends.at[2, k], ends.at[3, k], device,
             )
         for ri in range(2):
-            in_y[c, place.slab, part, ri] = out_z[
-                part, c, ri, pl.ds(thin * 8 * place.slab, thin * 8), :
+            in_y[place.slab, c, ri, pl.ds(part * thin * 8, thin * 8), :] = out_z[
+                c, ri, pl.ds(base + thin * 8 * place.slab, thin * 8), :
             ]
 
     @pl.loop(0, thin)
@@ -581,23 +717,24 @@
             while reach < width:
                 values = values + pltpu.roll(values, reach, 1)
                 reach *= 2
-            eta[z, cell * share : (cell + 1) * share, :] = values
-
-    base = gram(acc, 0, False, block, search, depth, lambda t: t)
-    base = gram(acc, base, True, search, search, depth, lambda t: t)
-    gram(acc, base, False, search, image, depth, lambda t: t)
+            local_eta[z, cell * share : (cell + 1) * share, :] = values
+
+    base = gram(second_acc, 0, False, block, search, depth, lambda t: t)
+    base = gram(second_acc, base, True, search, search, depth, lambda t: t)
+    gram(second_acc, base, False, search, image, depth, lambda t: t)
 
     for c in range(3):
         for part in range(parts):
             await_bytes(
-                in_y.at[c, pl.ds(0, slabs - 1), part], sems.at[3, part * 3 + c]
+                in_y.at[pl.ds(0, slabs - 1), c, :, pl.ds(0, thin * 8), :],
+                ends.at[3, part * 3 + c],
             )
 
         @pl.loop(0, thin)
         def _(z, c=c):
             stacked = jnp.concatenate(
                 [
-                    in_y[c, slab, part, ri, pl.ds(8 * z, 8), :]
+                    in_y[slab, c, ri, pl.ds(part * thin * 8 + 8 * z, 8), :]
                     for ri in range(2)
                     for slab in range(slabs)
                     for part in range(parts)
@@ -606,7 +743,7 @@
             )
             field = left_transform(y_plus, stacked)
             real, imag = field[:height], field[height:]
-            weight = eta[z]
+            weight = local_eta[z]
             real_weighted, imag_weighted = real * weight, imag * weight
             for shift in range(bands // 2 + 1):
                 if shift == 0:
@@ -619,21 +756,25 @@
                 for place_of, term in ((2 * shift, real_term), (2 * shift + 1, imag_term)):
                     field_acc[place_of] += jnp.sum(term.reshape(height // 8, 8, width), axis=0)
 
-    pieces = jnp.sum(field_acc[...], axis=1)
-    pieces = pltpu.roll(pieces, lax.rem(width - quarter * place.group, width), 1)
-    values = lane_sums(tile, acc)
-    message = jnp.concatenate([values, jnp.zeros((pieces.shape[0], values.shape[1]), jnp.float32)], 0)
+    fields = jnp.sum(field_acc[...], axis=1)
+    fields = pltpu.roll(fields, lax.rem(width - quarter * place.group, width), 1)
+    values = lane_sums(second_tile, second_acc)
     if values.shape[1] > width:
-        pieces = jnp.concatenate(
-            [pieces, jnp.zeros((pieces.shape[0], values.shape[1] - width), jnp.float32)], 1
-        )
-    message = jnp.concatenate([values, pieces], 0)
-    sums[...] = total(place, mine, first, second, tail, message)
+        empty = jnp.zeros((fields.shape[0], values.shape[1] - width), jnp.float32)
+        fields = jnp.concatenate([fields, empty], 1)
+    second_sums = total(
+        place, second_mine, second_slab, second_band, tail.at[1],
+        jnp.concatenate([values, fields], 0),
+    )
+    listed = pieces(first_sums, 0) + pieces(second_sums, 0)
+    for row in range(2 * (bands // 2 + 1)):
+        listed.append(second_sums[8 + row : 9 + row, :width])
+    results[...] = scatter(listed, result_sources, result_spread, result_gather) / cell_count
 
     @pl.loop(0, 3 * parts)
     def _(k):
-        await_bytes(in_z.at[0, 0, :, pl.ds(0, depth * 8 * (groups - 1)), :], sems.at[0, k])
-        await_bytes(in_y.at[0, pl.ds(0, slabs - 1), 0], sems.at[2, k])
+        await_bytes(in_z.at[0, :, pl.ds(0, depth * 8 * (groups - 1)), :], ends.at[0, k])
+        await_bytes(in_y.at[pl.ds(0, slabs - 1), 0, :, pl.ds(0, thin * 8), :], ends.at[2, k])
 
 
 def vmem(count):
@@ -644,165 +785,107 @@
     return -(-value // step) * step
 
 
-def first_operator(block, waves, depths, cells, groups, slabs):
+def step(block, materials, permittivity, bloch, groups, slabs):
     bands, _, _, depth, rows, width = block.shape
     half, height, length = depth // 2, rows * slabs, depth * groups
     share = height // (2 * groups)
-    count = 2 * gram_rows(bands, True)
-    lanes = round_up(count, width)
+    thin, parts, quarter = length // slabs, rows // 8, width // groups
     chunks = half // step_count(half)
-    single = lambda *shape: pltpu.VMEM(shape, jnp.float32)
-    tables = [
-        jnp.asarray(right_table(dft_matrix(width, 1.0).T)),
-        jnp.asarray(left_table(height, 1.0)),
-        jnp.asarray(left_table(length, 1.0)),
-        jnp.asarray(left_table(length, -1.0)),
-        jnp.asarray(left_table(height, -1.0)),
-        jnp.asarray(right_table(dft_matrix(width, -1.0).T)),
-    ]
-    return pl.pallas_call(
-        partial(first_kernel, groups, slabs),
-        in_specs=vmem(4 + len(tables)),
-        out_specs=vmem(2),
-        out_shape=[
-            jax.ShapeDtypeStruct(block.shape, jnp.float32),
-            jax.ShapeDtypeStruct((8, lanes), jnp.float32),
-        ],
-        scratch_shapes=[
-            single(2, 2, half, height, width),
-            single(2 * groups, 3, 2, half * share, width),
-            single(3, 2, length * share, width),
-            single(3, 2, length * share, width),
-            single(2 * groups, 3, 2, half * share, width),
-            single(length * share, width),
-            single(count, 8, width),
-            single(lanes, width),
-            single(2, 8, lanes),
-            single(slabs, 8, lanes),
-            single(groups, 8, lanes),
-            pltpu.SemaphoreType.DMA((8, chunks)),
-            pltpu.SemaphoreType.DMA((6,)),
-        ],
-        compiler_params=pltpu.CompilerParams(
-            collective_id=0, has_side_effects=True, vmem_limit_bytes=VMEM_LIMIT
-        ),
-    )(block, waves, depths, cells, *tables)
-
-
-def second_operator(mixing, block, image, waves, depths, cells, groups, slabs):
-    bands, _, _, depth, rows, width = block.shape
-    height, length = rows * slabs, depth * groups
-    thin, parts, quarter = length // slabs, rows // 8, width // groups
-    count = 2 * gram_rows(bands, False) + gram_rows(bands, True)
-    lanes = round_up(count, width)
+    first_count = 2 * gram_rows(bands, True)
+    first_lanes = round_up(first_count, width)
+    second_count = 2 * gram_rows(bands, False) + gram_rows(bands, True)
+    second_lanes = round_up(second_count, width)
     field_rows = round_up(2 * (bands // 2 + 1), 8)
-    message = (8 + field_rows, lanes)
-    single = lambda *shape: pltpu.VMEM(shape, jnp.float32)
+    message = (8 + field_rows, second_lanes)
+
     plain = dft_matrix(width, 1.0).T
     orders = []
     for band in range(bands):
         spots = np.arange(width) // quarter
         source = ((spots - band) % groups) * quarter + np.arange(width) % quarter
         orders.append(right_table(plain[:, np.concatenate([source, width + source])]))
+    first_pieces, second_pieces = first_lanes // width, second_lanes // width
+    solve_sources, *solve_tables = scatter_tables(system_entries(bands), first_pieces, width)
+    result_sources, *result_tables = scatter_tables(
+        result_entries(bands, width, first_pieces, second_pieces),
+        first_pieces + second_pieces + 2 * (bands // 2 + 1),
+        width,
+    )
     tables = [
-        jnp.asarray(np.stack(orders)),
-        jnp.asarray(left_table(length, 1.0)),
-        jnp.asarray(left_table(height, 1.0)),
+        right_table(plain),
+        np.stack(orders),
+        right_table(dft_matrix(width, -1.0).T),
+        left_table(height, 1.0),
+        left_table(height, -1.0),
+        left_table(length, 1.0),
+        left_table(length, -1.0),
+        *solve_tables,
+        *result_tables,
     ]
+    single = lambda *shape: pltpu.VMEM(shape, jnp.float32)
+    by_cell = (2 * groups, 3, 2, half * share, width)
+    by_part = (parts * groups, 3, 2, depth * 8, width)
+    out_x = [] if by_cell == by_part else [single(*by_part)]
+    kernel = partial(step_kernel, groups, slabs, solve_sources, result_sources)
+
+    def body(*refs):
+        refs = list(refs)
+        if not out_x:
+            outgoing = 2 + 2 + len(tables) + 2 + 2
+            refs.insert(outgoing + 4, refs[outgoing])
+        kernel(*refs)
+
     return pl.pallas_call(
-        partial(second_kernel, groups, slabs),
-        in_specs=[pl.BlockSpec(memory_space=pltpu.SMEM)] + vmem(5 + len(tables)),
+        body,
+        in_specs=[pl.BlockSpec(memory_space=pltpu.SMEM)] * 2 + vmem(2 + len(tables)),
         out_specs=vmem(2),
         out_shape=[
             jax.ShapeDtypeStruct(block.shape, jnp.float32),
-            jax.ShapeDtypeStruct(message, jnp.float32),
+            jax.ShapeDtypeStruct((result_tables[0].shape[0], width), jnp.float32),
         ],
         scratch_shapes=[
-            single(parts, groups, 3, 2, depth * 8, width),
-            single(parts, 3, 2, length * 8, width),
-            single(parts, 3, 2, length * 8, width),
-            single(3, slabs, parts, 2, thin * 8, width),
+            single(2, 2, half, height, width),
+            single(*block.shape),
+            single(*by_cell),
+            single(3, 2, length * share, width),
+            single(3, 2, length * share, width),
+            single(*by_cell),
+            *out_x,
+            single(length * share, width),
             single(thin, height, width),
-            single(count, 8, width),
+            single(2 * groups, thin * share, width),
+            single(3, height, width),
+            single(depth, 8, width),
+            single(2 * bands, bands, 8, width),
+            single(first_count, 8, width),
+            single(first_lanes, width),
+            single(2, 8, first_lanes),
+            single(slabs, 8, first_lanes),
+            single(groups, 8, first_lanes),
+            single(second_count, 8, width),
             single(field_rows, 8, width),
-            single(lanes, width),
+            single(second_lanes, width),
             single(2, *message),
             single(slabs, *message),
             single(groups, *message),
+            pltpu.SemaphoreType.DMA((8, chunks)),
             pltpu.SemaphoreType.DMA((4, 3 * parts)),
-            pltpu.SemaphoreType.DMA((4,)),
+            pltpu.SemaphoreType.DMA((3, 4)),
         ],
         compiler_params=pltpu.CompilerParams(
-            collective_id=1, has_side_effects=True, vmem_limit_bytes=VMEM_LIMIT
+            collective_id=0, has_side_effects=True, vmem_limit_bytes=VMEM_LIMIT
         ),
-    )(mixing, block, image, waves, depths, cells, *tables)
+    )(permittivity, bloch, block, materials, *[jnp.asarray(table) for table in tables])
 
 
 def shards(band_block, material_grid, inverse_permittivity, bloch_index):
     groups, slabs = lax.axis_size("band"), lax.axis_size("slab")
-    bands, _, _, depth, rows, width = band_block.shape
-    length, height = depth * groups, rows * slabs
-    grid_cells = length * height * width
-    thin = length // slabs
-    share = height // (2 * groups)
-    fraction = (bloch_index[0].astype(jnp.float32) + 1.0) / KPOINTS
-    width_wave = axis_values(width, 0.5, fraction, 0, width)[None, :]
-    height_wave = axis_values(height, 0.35, fraction, 0, height)[:, None]
-    planar = jnp.sqrt(width_wave * width_wave + height_wave * height_wave)
-    waves = jnp.stack([width_wave / planar, height_wave / planar, planar])
-    depth_wave = axis_values(length, 0.2, fraction, lax.axis_index("band") * depth, depth)
-    depths = jnp.broadcast_to(depth_wave[:, None, None], (depth, 8, width))
-    grouped = material_grid.reshape(thin, 2 * groups, share, width).transpose(1, 0, 2, 3)
-    grouped = grouped.reshape(2 * groups, thin * share, width)
-    cells = jnp.zeros(grouped.shape, jnp.float32)
-    for material in range(inverse_permittivity.shape[0]):
-        cells = jnp.where(grouped == material, inverse_permittivity[material] / grid_cells, cells)
-
-    image, sums = first_operator(band_block, waves, depths, cells, groups, slabs)
-    size = gram_rows(bands, True)
-    flat = sums[0] / grid_cells
-    own_real, own_imag = unpack(flat[:size], bands, True)
-    cross_real, cross_imag = unpack(flat[size : 2 * size], bands, True)
-    join = lambda rows: jnp.concatenate([jnp.concatenate(row, 1) for row in rows], 0)
-    system = join([[own_real, -own_imag], [own_imag, own_real]])
-    right_side = jnp.concatenate([cross_real, cross_imag], 0)
-    factor = jnp.linalg.cholesky(system)
-    mixing = jax.scipy.linalg.cho_solve((factor, True), right_side)
-
-    by_slab = waves.reshape(3, slabs, rows, width).transpose(1, 0, 2, 3)
-    search_block, sums = second_operator(
-        mixing, band_block, image, by_slab, depths, cells, groups, slabs
-    )
-    sums = sums / grid_cells
-    size = 2 * bands * bands
-    flat = sums[0]
-    mixed_real, mixed_imag = unpack(flat[:size], bands, False)
-    search_real, search_imag = unpack(flat[size : size + gram_rows(bands, True)], bands, True)
-    flat = flat[size + gram_rows(bands, True) :]
-    back_real, back_imag = unpack(flat[:size], bands, False)
-    field = sums[8:, :width].reshape(-1, groups, width // groups).sum(2)
-    real = [[None] * bands for _ in range(bands)]
-    imag = [[None] * bands for _ in range(bands)]
-    for i in range(bands):
-        for shift in range(bands // 2 + 1):
-            j = (i - shift) % bands
-            real[i][j], imag[i][j] = field[2 * shift, i], field[2 * shift + 1, i]
-            real[j][i], imag[j][i] = real[i][j], -imag[i][j]
-    stack = lambda rows: jnp.stack([jnp.stack(row) for row in rows])
-    field_real, field_imag = stack(real), stack(imag)
-    correlation = jnp.stack(
-        [
-            join([[own_real, mixed_real], [mixed_real.T, search_real]]),
-            join([[own_imag, mixed_imag], [-mixed_imag.T, search_imag]]),
-        ]
-    )
-    projected = jnp.stack(
-        [
-            join([[cross_real, back_real.T], [back_real, field_real]]),
-            join([[cross_imag, -back_imag.T], [back_imag, field_imag]]),
-        ]
-    )
-    return (search_block, correlation, projected)
+    size = 2 * band_block.shape[0]
+    search_block, results = step(
+        band_block, material_grid, inverse_permittivity, bloch_index, groups, slabs
+    )
+    results = results[:, :size].reshape(2, 2, size, size)
+    return (search_block, results[0], results[1])
 
 
 def solution(mesh):

time: 587 us -> 430 us (0.73)
  other arithmetic: 116 us -> 0 us
  between operations: 21.8 us -> 1.29 us
  local copies, waits for them, and re-layouts: 17.1 us -> 5.92 us
  Pallas kernels: 429 us -> 422 us
    another operation x60 -> x0, other arithmetic: 112 us -> none  [the longest x42 92.3 us: unpack(): stack = lambda rows: jnp.stack([jnp.stack(row) for row in rows])]
    slice x12 -> x0, local copies, waits for them, and re-layouts: 8.53 us -> none  [the longest x8 5.69 us: unpack(): real[i][j], imag[i][j] = (flat[place], flat[place + 1])]
    pallas_call x2 -> x1, Pallas kernels: 429 us -> 422 us  [step(): pl.pallas_call(body, in_specs=[pl.BlockSpec(memory_space=pltpu.SMEM)] * 2...]
where the time goes in v2:
time: 430 us; the launch traced here: 429 us
  Pallas kernels  422 us (98%)
  local copies, waits for them, and re-layouts  5.92 us (1%)
    pallas_call x1, Pallas kernels, step(): pl.pallas_call(body, in_specs=[pl.BlockSpec(memory_space=pltpu.SMEM)] * 2...  422 us

profile of v2, /device:TPU:0, one launch (start us, length us, event | category | flops | bytes accessed | tf_op | source)
XLA Modules:
  0.0 429.4 jit_solution(8447551695767663597)
XLA Ops:
  1.3 422.2 %shard_map.166 = (f32[4,2,2,32,16,128]{5,4,3,2,1,0:T(8,128)}, f32[32,128]{1,0:T(8,128)}) custom-call(f32[4]{0:T(128)} %refs_0_.1, s32[1]{0:T(128)S(6)} %copy.25.refs_1_, f32[4,2,2,32,16,128]{5,4,3,2,1,0:T(8,128)} %refs_2_.1, s32[16,128,128]{2,1,0:T(8,128)} %refs_3_.1, bf16[768,256]{1,0:T(8,128)(2,1)} %constant.18.clone.refs_4_, ...), custom_call_target="tpu_custom_call" | custom-call | tf_op jit(solution)/shard_map/pallas_call | solution.py:838
  423.5 1.3 slice_bitcast_fusion
  424.8 4.6 %copy.26 = f32[4,2,2,32,16,128]{5,4,3,2,1,0:T(8,128)} copy(f32[4,2,2,32,16,128]{5,4,3,2,1,0:T(8,128)} %get-tuple-element.15) | data formatting | bytes 8388608

commit v3 on v2

--- a/solution.py
+++ b/solution.py
@@ -12,7 +12,8 @@
 KPOINTS = 8
 HIGHEST = lax.Precision.HIGHEST
 MESH = pl.DeviceIdType.MESH
-VMEM_LIMIT = 60 * 1024 * 1024
+VMEM_LIMIT = 54 * 1024 * 1024
+WINDOW = 3
 
 
 def halves(values):
@@ -58,10 +59,6 @@
 def right_transform(values, table):
     high, low = halves(values)
     return dot(jnp.concatenate([high, low, high], 1), table[...])
-
-
-def step_count(size):
-    return 2 if size % 2 == 0 else 1
 
 
 def gram(acc, base, hermitian, left, right, count, depth_of):
@@ -305,15 +302,20 @@
 
 
 def step_kernel(
-    groups, slabs, solve_sources, result_sources,
-    permittivity, bloch, block, materials, x_plus, x_split, x_minus, y_plus, y_minus, z_plus,
-    z_minus, solve_spread, solve_gather, result_spread, result_gather,
-    search, results,
-    work, image, out_y, in_z, out_z, in_y, out_x, eta, local_eta, cells, waves, depths, mixing,
-    first_acc, first_tile, first_mine, first_slab, first_band,
-    second_acc, field_acc, second_tile, second_mine, second_slab, second_band,
-    sems, ends, tail,
+    groups, slabs, arrays, solve_sources, result_sources,
+    permittivity, bloch, given, *refs,
 ):
+    outside, refs = (given, *refs[: arrays - 1]), refs[arrays - 1 :]
+    (search, results), inside, refs = refs[:2], refs[2 : arrays + 2], refs[arrays + 2 :]
+    block, materials, x_split, x_minus, y_plus, y_minus = inside[:6]
+    z_plus, z_minus = inside[6:8] if arrays == 12 else (y_plus, y_minus)
+    solve_spread, solve_gather, result_spread, result_gather = inside[-4:]
+    (
+        work, image, out_y, in_z, out_z, in_y, out_x, eta, local_eta, cells, waves, depths, mixing,
+        first_acc, first_tile, first_mine, first_slab, first_band,
+        second_acc, field_acc, second_tile, second_mine, second_slab, second_band,
+        sems, comes, ends, tail, loads,
+    ) = refs
     place = Place(groups, slabs)
     bands, _, _, depth, rows, width = block.shape
     half = depth // 2
@@ -321,9 +323,10 @@
     length = depth * groups
     share = out_y.shape[3] // half
     cell_count = length * height * width
-    step = step_count(half)
-    chunks = half // step
-    part = step * share
+    thin = length // slabs
+    chunks = half
+    parts = share // 8
+    lead = min(WINDOW, chunks)
 
     enter(
         [place.slab_peer(i)[1] for i in range(1, slabs)]
@@ -334,34 +337,49 @@
         ]
     )
 
-    @pl.loop(0, chunks)
-    def _(k):
+    for place_of, (source, target) in enumerate(zip(outside, inside)):
+        pltpu.make_async_copy(source, target, loads.at[place_of]).start()
+
+    def send_out(k):
         for i in range(1, slabs):
             slab, device = place.slab_peer(i)
             send(
-                block.at[slab // 2, :, :, pl.ds(half * (slab % 2) + k * step, step), :, :],
-                work.at[:, :, pl.ds(k * step, step), pl.ds(rows * place.slab, rows), :],
+                given.at[slab // 2, :, :, pl.ds(half * (slab % 2) + k, 1), :, :],
+                work.at[:, :, pl.ds(k, 1), pl.ds(rows * place.slab, rows), :],
                 sems.at[0, k], sems.at[1, k], device,
             )
 
-    @pl.loop(0, length // slabs)
+    @pl.loop(0, lead)
+    def _(k):
+        send_out(k)
+
+    for place_of, (source, target) in enumerate(zip(outside, inside)):
+        pltpu.make_async_copy(source, target, loads.at[place_of]).wait()
+
+    @pl.loop(0, thin)
     def _(z):
         for cell in range(2 * groups):
-            found = materials[z, cell * share : (cell + 1) * share, :]
-            values = jnp.zeros(found.shape, jnp.float32)
-            for material in range(permittivity.shape[0]):
-                values = jnp.where(found == material, permittivity[material] / cell_count, values)
-            cells[cell, pl.ds(z * share, share), :] = values
-
-    slab_cells = cells.shape[1]
-    for i in range(1, slabs):
-        slab, device = place.slab_peer(i)
-        send(
-            cells.at[2 * place.group + slab % 2],
-            eta.at[pl.ds(slab_cells * place.slab, slab_cells), :],
-            tail.at[2, 0], tail.at[2, 1], device,
-        )
-    eta[pl.ds(slab_cells * place.slab, slab_cells), :] = cells[place.cell]
+            for part in range(parts):
+                found = materials[z, pl.ds(cell * share + part * 8, 8), :]
+                values = jnp.zeros(found.shape, jnp.float32)
+                for material in range(permittivity.shape[0]):
+                    values = jnp.where(found == material, permittivity[material] / cell_count, values)
+                cells[cell, pl.ds((part * thin + z) * 8, 8), :] = values
+
+    def send_cells():
+        for part in range(parts):
+            target = pl.ds((part * length + thin * place.slab) * 8, thin * 8)
+            for i in range(1, slabs):
+                slab, device = place.slab_peer(i)
+                send(
+                    cells.at[2 * place.group + slab % 2, pl.ds(part * thin * 8, thin * 8), :],
+                    eta.at[target, :],
+                    tail.at[2, part], tail.at[3, part], device,
+                )
+
+    for part in range(parts):
+        target = pl.ds((part * length + thin * place.slab) * 8, thin * 8)
+        eta[target, :] = cells[place.cell, pl.ds(part * thin * 8, thin * 8), :]
 
     fraction = (bloch[0].astype(jnp.float32) + 1.0) / KPOINTS
     at_x = lax.broadcasted_iota(jnp.int32, (height, width), 1)
@@ -379,184 +397,209 @@
     gram(first_acc, 0, True, block, block, depth, lambda t: t)
 
     @pl.loop(0, chunks)
-    def _(k):
+    def _(z):
         await_bytes(
-            work.at[:, :, pl.ds(0, step), pl.ds(0, rows * (slabs - 1)), :], sems.at[1, k]
+            work.at[:, :, pl.ds(0, 1), pl.ds(0, rows * (slabs - 1)), :], sems.at[1, z]
         )
 
-        @pl.loop(0, step)
-        def _(i):
-            z = k * step + i
-            for comp in range(2):
-                for ri in range(2):
-                    work[comp, ri, z, pl.ds(rows * place.slab, rows), :] = block[
-                        place.layer, comp, ri, half * place.core + z
-                    ]
-            across, along, planar = waves[0], waves[1], waves[2]
-            deep = depths[half * place.core + z, 0:1, :]
-            size = jnp.sqrt(planar * planar + deep * deep)
-            fields = []
+        @pl.when(z + lead < chunks)
+        def _():
+            send_out(z + lead)
+
+        @pl.when(z == chunks - 1)
+        def _():
+            send_cells()
+
+        for comp in range(2):
             for ri in range(2):
-                one = work[0, ri, z]
-                two = work[1, ri, z] * size
-                upright = one * deep
-                fields.append(
-                    [across * upright - along * two, along * upright + across * two, -planar * one]
+                work[comp, ri, z, pl.ds(rows * place.slab, rows), :] = block[
+                    place.layer, comp, ri, half * place.core + z
+                ]
+        across, along, planar = waves[0], waves[1], waves[2]
+        deep = depths[half * place.core + z, 0:1, :]
+        size = jnp.sqrt(planar * planar + deep * deep)
+        fields = []
+        for ri in range(2):
+            one = work[0, ri, z]
+            two = work[1, ri, z] * size
+            upright = one * deep
+            fields.append(
+                [across * upright - along * two, along * upright + across * two, -planar * one]
+            )
+        curled = jnp.concatenate(
+            [jnp.concatenate([fields[0][c], fields[1][c]], 1) for c in range(3)], 0
+        )
+        lines = right_transform(curled, x_split.at[0])
+        stacked = jnp.concatenate(
+            [
+                jnp.concatenate(
+                    [
+                        lines[c * height : (c + 1) * height, :width],
+                        lines[c * height : (c + 1) * height, width:],
+                    ],
+                    0,
                 )
-            curled = jnp.concatenate(
-                [jnp.concatenate([fields[0][c], fields[1][c]], 1) for c in range(3)], 0
-            )
-            lines = right_transform(curled, x_plus)
-            stacked = jnp.concatenate(
-                [
-                    jnp.concatenate(
-                        [
-                            lines[c * height : (c + 1) * height, :width],
-                            lines[c * height : (c + 1) * height, width:],
-                        ],
-                        0,
-                    )
-                    for c in range(3)
-                ],
-                1,
-            )
-            planes = left_transform(y_plus, stacked)
+                for c in range(3)
+            ],
+            1,
+        )
+        planes = left_transform(y_plus, stacked)
+        for c in range(3):
+            for ri in range(2):
+                for cell in range(2 * groups):
+                    for part in range(parts):
+                        base = ri * height + cell * share + part * 8
+                        out_y[cell, c, ri, pl.ds((part * half + z) * 8, 8), :] = planes[
+                            base : base + 8, c * width : (c + 1) * width
+                        ]
+
+        for part in range(parts):
+            source = pl.ds((part * half + z) * 8, 8)
+            target = pl.ds((part * length + place.cell * half + z) * 8, 8)
+            for i in range(1, 2 * groups):
+                cell, device = place.plane_peer(i)
+                send(
+                    out_y.at[cell, :, :, source, :],
+                    in_z.at[:, :, target, :],
+                    sems.at[2, z], comes.at[part, z], device,
+                )
             for c in range(3):
                 for ri in range(2):
-                    for cell in range(2 * groups):
-                        base = ri * height + cell * share
-                        out_y[cell, c, ri, pl.ds(z * share, share), :] = planes[
-                            base : base + share, c * width : (c + 1) * width
-                        ]
-
+                    in_z[c, ri, target, :] = out_y[place.cell, c, ri, source, :]
+
+    def columns_of(source, c, first):
+        return jnp.concatenate(
+            [
+                jnp.concatenate(
+                    [source[c, ri, pl.ds(first + j, length, stride=8), :] for ri in range(2)], 0
+                )
+                for j in range(2)
+            ],
+            1,
+        )
+
+    def keep_columns(target, c, first, values):
+        for j in range(2):
+            for ri in range(2):
+                target[c, ri, pl.ds(first + j, length, stride=8), :] = values[
+                    ri * length : (ri + 1) * length, j * width : (j + 1) * width
+                ]
+
+    for part in range(parts):
+        @pl.loop(0, chunks)
+        def _(k, part=part):
+            await_bytes(in_z.at[:, :, pl.ds(0, 8 * (2 * groups - 1)), :], comes.at[part, k])
+
+        @pl.loop(0, 4)
+        def _(pair, part=part):
+            first = part * length * 8 + 2 * pair
+            for c in range(3):
+                keep_columns(in_z, c, first, left_transform(z_plus, columns_of(in_z, c, first)))
+
+    def send_back(k, part):
         for i in range(1, 2 * groups):
             cell, device = place.plane_peer(i)
             send(
-                out_y.at[cell, :, :, pl.ds(k * part, part), :],
-                in_z.at[:, :, pl.ds(place.cell * half * share + k * part, part), :],
-                sems.at[2, k], sems.at[3, k], device,
+                out_z.at[:, :, pl.ds((part * length + cell * half + k) * 8, 8), :],
+                in_y.at[place.cell, :, :, pl.ds((part * half + k) * 8, 8), :],
+                sems.at[4, k], sems.at[5, k], device,
             )
+
+    for part in range(parts):
+        await_bytes(eta.at[pl.ds(0, thin * 8 * (slabs - 1)), :], tail.at[3, part])
+
+        @pl.loop(0, 4)
+        def _(pair, part=part):
+            first = part * length * 8 + 2 * pair
+            weight = jnp.concatenate(
+                [eta[pl.ds(first + j, length, stride=8), :] for j in range(2)], 1
+            )
+            weight = jnp.concatenate([weight, weight], 0)
+            for c in range(3):
+                field = columns_of(in_z, c, first) * weight
+                keep_columns(out_z, c, first, left_transform(z_minus, field))
+
+        @pl.loop(0, lead)
+        def _(k, part=part):
+            send_back(k, part)
+
+    @pl.loop(0, chunks)
+    def _(z):
         for c in range(3):
             for ri in range(2):
-                in_z[c, ri, pl.ds(place.cell * half * share + k * part, part), :] = out_y[
-                    place.cell, c, ri, pl.ds(k * part, part), :
+                for part in range(parts):
+                    in_y[place.cell, c, ri, pl.ds((part * half + z) * 8, 8), :] = out_z[
+                        c, ri, pl.ds((part * length + place.cell * half + z) * 8, 8), :
+                    ]
+        await_bytes(in_y.at[pl.ds(0, 2 * groups - 1), :, :, pl.ds(0, share), :], sems.at[5, z])
+
+        @pl.when(z + lead < chunks)
+        def _():
+            for part in range(parts):
+                send_back(z + lead, part)
+
+
+        stacked = jnp.concatenate(
+            [
+                jnp.concatenate(
+                    [
+                        in_y[cell, c, ri, pl.ds((part * half + z) * 8, 8), :]
+                        for ri in range(2)
+                        for cell in range(2 * groups)
+                        for part in range(parts)
+                    ],
+                    0,
+                )
+                for c in range(3)
+            ],
+            1,
+        )
+        planes = left_transform(y_minus, stacked)
+        lines = jnp.concatenate(
+            [
+                jnp.concatenate(
+                    [
+                        planes[:height, c * width : (c + 1) * width],
+                        planes[height:, c * width : (c + 1) * width],
+                    ],
+                    1,
+                )
+                for c in range(3)
+            ],
+            0,
+        )
+        curled = right_transform(lines, x_minus)
+        across, along, planar = waves[0], waves[1], waves[2]
+        deep = depths[half * place.core + z, 0:1, :]
+        size = jnp.sqrt(planar * planar + deep * deep)
+        for ri in range(2):
+            fields = [
+                curled[c * height : (c + 1) * height, ri * width : (ri + 1) * width]
+                for c in range(3)
+            ]
+            work[0, ri, z] = deep * (across * fields[0] + along * fields[1]) - planar * fields[2]
+            work[1, ri, z] = size * (across * fields[1] - along * fields[0])
+        for comp in range(2):
+            for ri in range(2):
+                image[place.layer, comp, ri, half * place.core + z] = work[
+                    comp, ri, z, pl.ds(rows * place.slab, rows), :
                 ]
-
-    await_bytes(eta.at[pl.ds(0, slab_cells * (slabs - 1)), :], tail.at[2, 1])
-
-    @pl.loop(0, chunks)
-    def _(k):
-        await_bytes(in_z.at[:, :, pl.ds(0, part * (2 * groups - 1)), :], sems.at[3, k])
-
-    @pl.loop(0, share // 2)
-    def _(pair):
-        weights = [eta[pl.ds(2 * pair + j, length, stride=share), :] for j in range(2)]
-        for c in range(3):
-            stacked = jnp.concatenate(
-                [
-                    jnp.concatenate(
-                        [in_z[c, ri, pl.ds(2 * pair + j, length, stride=share), :] for ri in range(2)],
-                        0,
-                    )
-                    for j in range(2)
-                ],
-                1,
-            )
-            field = left_transform(z_plus, stacked)
-            weight = jnp.concatenate(weights, 1)
-            field = field * jnp.concatenate([weight, weight], 0)
-            back = left_transform(z_minus, field)
-            for j in range(2):
-                for ri in range(2):
-                    out_z[c, ri, pl.ds(2 * pair + j, length, stride=share), :] = back[
-                        ri * length : (ri + 1) * length, j * width : (j + 1) * width
-                    ]
-
-    @pl.loop(0, chunks)
-    def _(k):
-        for i in range(1, 2 * groups):
-            cell, device = place.plane_peer(i)
-            send(
-                out_z.at[:, :, pl.ds(cell * half * share + k * part, part), :],
-                in_y.at[place.cell, :, :, pl.ds(k * part, part), :],
-                sems.at[4, k], sems.at[5, k], device,
-            )
-
-    @pl.loop(0, chunks)
-    def _(k):
-        for c in range(3):
-            for ri in range(2):
-                in_y[place.cell, c, ri, pl.ds(k * part, part), :] = out_z[
-                    c, ri, pl.ds(place.cell * half * share + k * part, part), :
-                ]
-        await_bytes(
-            in_y.at[pl.ds(0, 2 * groups - 1), :, :, pl.ds(0, part), :], sems.at[5, k]
-        )
-
-        @pl.loop(0, step)
-        def _(i):
-            z = k * step + i
-            stacked = jnp.concatenate(
-                [
-                    jnp.concatenate(
-                        [
-                            in_y[cell, c, ri, pl.ds(z * share, share), :]
-                            for ri in range(2)
-                            for cell in range(2 * groups)
-                        ],
-                        0,
-                    )
-                    for c in range(3)
-                ],
-                1,
-            )
-            planes = left_transform(y_minus, stacked)
-            lines = jnp.concatenate(
-                [
-                    jnp.concatenate(
-                        [
-                            planes[:height, c * width : (c + 1) * width],
-                            planes[height:, c * width : (c + 1) * width],
-                        ],
-                        1,
-                    )
-                    for c in range(3)
-                ],
-                0,
-            )
-            curled = right_transform(lines, x_minus)
-            across, along, planar = waves[0], waves[1], waves[2]
-            deep = depths[half * place.core + z, 0:1, :]
-            size = jnp.sqrt(planar * planar + deep * deep)
-            for ri in range(2):
-                fields = [
-                    curled[c * height : (c + 1) * height, ri * width : (ri + 1) * width]
-                    for c in range(3)
-                ]
-                work[0, ri, z] = deep * (across * fields[0] + along * fields[1]) - planar * fields[2]
-                work[1, ri, z] = size * (across * fields[1] - along * fields[0])
-            for comp in range(2):
-                for ri in range(2):
-                    image[place.layer, comp, ri, half * place.core + z] = work[
-                        comp, ri, z, pl.ds(rows * place.slab, rows), :
-                    ]
 
         for i in range(1, slabs):
             slab, device = place.slab_peer(i)
             send(
-                work.at[:, :, pl.ds(k * step, step), pl.ds(rows * slab, rows), :],
-                image.at[place.layer, :, :, pl.ds(half * place.core + k * step, step), :, :],
-                sems.at[6, k], sems.at[7, k], device,
+                work.at[:, :, pl.ds(z, 1), pl.ds(rows * slab, rows), :],
+                image.at[place.layer, :, :, pl.ds(half * place.core + z, 1), :, :],
+                sems.at[6, z], sems.at[7, z], device,
             )
 
     @pl.loop(0, chunks)
     def _(k):
         await_bytes(
-            work.at[:, :, pl.ds(0, step), pl.ds(0, rows * (slabs - 1)), :], sems.at[7, k]
+            work.at[:, :, pl.ds(0, 1), pl.ds(0, rows * (slabs - 1)), :], sems.at[7, k]
         )
         gram(
-            first_acc, gram_rows(bands, True), True, block, image, 2 * step,
-            lambda t: half * (t // step) + k * step + t % step,
+            first_acc, gram_rows(bands, True), True, block, image, 2, lambda t: half * t + k,
         )
 
     first_sums = total(place, first_mine, first_slab, first_band, tail.at[0], lane_sums(first_tile, first_acc))
@@ -574,22 +617,31 @@
 
     @pl.loop(0, chunks)
     def _(k):
-        slab_bytes = work.at[:, :, pl.ds(0, step), pl.ds(0, rows * (slabs - 1)), :]
-        plane_bytes = in_z.at[:, :, pl.ds(0, part * (2 * groups - 1)), :]
+        slab_bytes = work.at[:, :, pl.ds(0, 1), pl.ds(0, rows * (slabs - 1)), :]
+        plane_bytes = in_z.at[:, :, pl.ds(0, share * (2 * groups - 1)), :]
         await_bytes(slab_bytes, sems.at[0, k])
         await_bytes(plane_bytes, sems.at[2, k])
         await_bytes(plane_bytes, sems.at[4, k])
         await_bytes(slab_bytes, sems.at[6, k])
 
-    await_bytes(eta.at[pl.ds(0, slab_cells * (slabs - 1)), :], tail.at[2, 0])
-
-    parts = rows // 8
-    thin = length // slabs
+    for part in range(parts):
+        await_bytes(eta.at[pl.ds(0, thin * 8 * (slabs - 1)), :], tail.at[2, part])
+
     quarter = width // groups
     second_acc[...] = jnp.zeros_like(second_acc)
     field_acc[...] = jnp.zeros_like(field_acc)
     lane = lax.broadcasted_iota(jnp.int32, (1, width), 1) // quarter
     deep_step = 8 if depth % 8 == 0 else 1
+
+    def send_quarter(k):
+        part, c = k // 3, k % 3
+        for i in range(1, groups):
+            group, device = place.band_peer(i)
+            send(
+                out_x.at[part * groups + group, c],
+                in_z.at[c, :, pl.ds((part * length + depth * place.group) * 8, depth * 8), :],
+                ends.at[0, k], ends.at[1, k], device,
+            )
 
     @pl.loop(0, parts)
     def _(part):
@@ -655,45 +707,34 @@
                         out_x[part * groups + target, c, ri, at, :] = packed[c * count : (c + 1) * count]
 
         for c in range(3):
-            for i in range(1, groups):
-                group, device = place.band_peer(i)
-                send(
-                    out_x.at[part * groups + group, c],
-                    in_z.at[c, :, pl.ds((part * length + depth * place.group) * 8, depth * 8), :],
-                    ends.at[0, part * 3 + c], ends.at[1, part * 3 + c], device,
-                )
             for ri in range(2):
                 in_z[c, ri, pl.ds((part * length + depth * place.group) * 8, depth * 8), :] = out_x[
                     part * groups + place.group, c, ri
                 ]
 
+        @pl.when(part == 0)
+        def _():
+            send_quarter(0)
+
     @pl.loop(0, 3 * parts)
     def _(k):
         part, c = k // 3, k % 3
         await_bytes(in_z.at[c, :, pl.ds(0, depth * 8 * (groups - 1)), :], ends.at[1, k])
+
+        @pl.when(k == 0)
+        def _():
+            send_quarter(1)
+
+        @pl.when(k + 2 < 3 * parts)
+        def _():
+            send_quarter(k + 2)
+
         base = part * length * 8
 
         @pl.loop(0, 4)
         def _(pair):
-            stacked = jnp.concatenate(
-                [
-                    jnp.concatenate(
-                        [
-                            in_z[c, ri, pl.ds(base + 2 * pair + j, length, stride=8), :]
-                            for ri in range(2)
-                        ],
-                        0,
-                    )
-                    for j in range(2)
-                ],
-                1,
-            )
-            columns = left_transform(z_plus, stacked)
-            for j in range(2):
-                for ri in range(2):
-                    out_z[c, ri, pl.ds(base + 2 * pair + j, length, stride=8), :] = columns[
-                        ri * length : (ri + 1) * length, j * width : (j + 1) * width
-                    ]
+            first = base + 2 * pair
+            keep_columns(out_z, c, first, left_transform(z_plus, columns_of(in_z, c, first)))
 
         for i in range(1, slabs):
             slab, device = place.slab_peer(i)
@@ -710,14 +751,15 @@
     @pl.loop(0, thin)
     def _(z):
         for cell in range(2 * groups):
-            values = cells[cell, pl.ds(z * share, share), :]
-            values = pltpu.roll(values, lax.rem(width - quarter * place.group, width), 1)
-            values = jnp.where(lane == 0, values, 0.0)
-            reach = quarter
-            while reach < width:
-                values = values + pltpu.roll(values, reach, 1)
-                reach *= 2
-            local_eta[z, cell * share : (cell + 1) * share, :] = values
+            for part in range(parts):
+                values = cells[cell, pl.ds((part * thin + z) * 8, 8), :]
+                values = pltpu.roll(values, lax.rem(width - quarter * place.group, width), 1)
+                values = jnp.where(lane == 0, values, 0.0)
+                reach = quarter
+                while reach < width:
+                    values = values + pltpu.roll(values, reach, 1)
+                    reach *= 2
+                local_eta[z, cell * share + part * 8 : cell * share + part * 8 + 8, :] = values
 
     base = gram(second_acc, 0, False, block, search, depth, lambda t: t)
     base = gram(second_acc, base, True, search, search, depth, lambda t: t)
@@ -790,7 +832,7 @@
     half, height, length = depth // 2, rows * slabs, depth * groups
     share = height // (2 * groups)
     thin, parts, quarter = length // slabs, rows // 8, width // groups
-    chunks = half // step_count(half)
+    chunks = half
     first_count = 2 * gram_rows(bands, True)
     first_lanes = round_up(first_count, width)
     second_count = 2 * gram_rows(bands, False) + gram_rows(bands, True)
@@ -812,13 +854,11 @@
         width,
     )
     tables = [
-        right_table(plain),
         np.stack(orders),
         right_table(dft_matrix(width, -1.0).T),
         left_table(height, 1.0),
         left_table(height, -1.0),
-        left_table(length, 1.0),
-        left_table(length, -1.0),
+        *([] if length == height else [left_table(length, 1.0), left_table(length, -1.0)]),
         *solve_tables,
         *result_tables,
     ]
@@ -826,24 +866,27 @@
     by_cell = (2 * groups, 3, 2, half * share, width)
     by_part = (parts * groups, 3, 2, depth * 8, width)
     out_x = [] if by_cell == by_part else [single(*by_part)]
-    kernel = partial(step_kernel, groups, slabs, solve_sources, result_sources)
+    kernel = partial(
+        step_kernel, groups, slabs, 2 + len(tables), solve_sources, result_sources
+    )
 
     def body(*refs):
         refs = list(refs)
         if not out_x:
-            outgoing = 2 + 2 + len(tables) + 2 + 2
+            outgoing = 2 + 2 * (2 + len(tables)) + 2 + 2
             refs.insert(outgoing + 4, refs[outgoing])
         kernel(*refs)
 
     return pl.pallas_call(
         body,
-        in_specs=[pl.BlockSpec(memory_space=pltpu.SMEM)] * 2 + vmem(2 + len(tables)),
+        in_specs=[pl.BlockSpec(memory_space=pltpu.SMEM)] * 2 + [pl.BlockSpec(memory_space=pl.ANY)] * (2 + len(tables)),
         out_specs=vmem(2),
         out_shape=[
-            jax.ShapeDtypeStruct(block.shape, jnp.float32),
+            pltpu.VMEM(block.shape, jnp.float32),
             jax.ShapeDtypeStruct((result_tables[0].shape[0], width), jnp.float32),
         ],
         scratch_shapes=[
+            *[pltpu.VMEM(array.shape, array.dtype) for array in (block, materials, *tables)],
             single(2, 2, half, height, width),
             single(*block.shape),
             single(*by_cell),
@@ -869,8 +912,10 @@
             single(slabs, *message),
             single(groups, *message),
             pltpu.SemaphoreType.DMA((8, chunks)),
+            pltpu.SemaphoreType.DMA((parts, chunks)),
             pltpu.SemaphoreType.DMA((4, 3 * parts)),
-            pltpu.SemaphoreType.DMA((3, 4)),
+            pltpu.SemaphoreType.DMA((4, 4)),
+            pltpu.SemaphoreType.DMA((2 + len(tables),)),
         ],
         compiler_params=pltpu.CompilerParams(
             collective_id=0, has_side_effects=True, vmem_limit_bytes=VMEM_LIMIT

time: 430 us -> 401 us (0.933)
  Pallas kernels: 422 us -> 397 us
    pallas_call x1, Pallas kernels: 422 us -> 397 us  [step(): pl.pallas_call(body, in_specs=[pl.BlockSpec(memory_space=pltpu.SMEM)] * 2...]
where the time goes in v3:
time: 401 us
  Pallas kernels  397 us (99%)
    pallas_call x1, Pallas kernels, step(): pl.pallas_call(body, in_specs=[pl.BlockSpec(memory_space=pltpu.SMEM)] * 2...  397 us

profile of v3, /device:TPU:0, one launch (start us, length us, event | category | flops | bytes accessed | tf_op | source)
XLA Modules:
  0.0 401.2 jit_solution(16324779859895686734)
XLA Ops:
  1.3 397.3 %shard_map.139 = (f32[4,2,2,32,16,128]{5,4,3,2,1,0:T(8,128)S(1)}, f32[32,128]{1,0:T(8,128)}) custom-call(f32[4]{0:T(128)} %refs_0_.1, s32[1]{0:T(128)S(6)} %copy.23.refs_1_, f32[4,2,2,32,16,128]{5,4,3,2,1,0:T(8,128)} %refs_2_.1, s32[16,128,128]{2,1,0:T(8,128)} %refs_3_.1, bf16[4,768,256]{2,1,0:T(8,128)(2,1)} %constant.16.clone.refs_4_, ...), custom_call_target="tpu_custom_call" | custom-call | tf_op jit(solution)/shard_map/pallas_call | solution.py:880
  398.6 0.0 copy-start
  398.6 2.0 copy.22
  400.6 0.0 copy-done
  400.6 0.6 slice_bitcast_fusion
Async XLA Ops:
  398.6 2.0 copy-start

commit v4 on v3

--- a/solution.py
+++ b/solution.py
@@ -40,8 +40,7 @@
 
 
 def right_table(matrix):
-    high, low = numpy_halves(matrix)
-    return np.concatenate([high, high, low], 0)
+    return np.concatenate(numpy_halves(matrix), 0)
 
 
 def dot(left, right):
@@ -57,8 +56,9 @@
 
 
 def right_transform(values, table):
+    size = values.shape[1]
     high, low = halves(values)
-    return dot(jnp.concatenate([high, low, high], 1), table[...])
+    return dot(jnp.concatenate([high, high], 1), table[...]) + dot(low, table[:size, :])
 
 
 def gram(acc, base, hermitian, left, right, count, depth_of):
@@ -161,10 +161,12 @@
             return (bands + i, i, bands + j, -sign)
 
         entries += complex_entries(0, 0, pairs, lambda i, j: mirrored(i, j, left))
-    right = lambda i, j, sign: (i, bands + i, 2 * bands + j, sign)
-    return entries + complex_entries(
-        0, gram_rows(bands, True), pairs, lambda i, j: mirrored(i, j, right)
-    )
+    return entries
+
+
+def side_entries(bands):
+    right = lambda i, j, sign: (i, bands + i, j, sign)
+    return complex_entries(0, 0, pair_list(bands, True), lambda i, j: mirrored(i, j, right))
 
 
 def result_entries(bands, width, first_pieces, second_pieces):
@@ -178,9 +180,9 @@
 
     entries = complex_entries(0, 0, own, lambda i, j: mirrored(i, j, spot(0, 0, 0)))
     entries += complex_entries(
-        0, gram_rows(bands, True), own, lambda i, j: mirrored(i, j, spot(1, 0, 0))
-    )
-    source, base = first_pieces, 0
+        first_pieces, 0, own, lambda i, j: mirrored(i, j, spot(1, 0, 0))
+    )
+    source, base = 2 * first_pieces, 0
     entries += complex_entries(
         source, base, every,
         lambda i, j: [spot(0, 0, bands)(i, j, 1.0), spot(0, bands, 0)(j, i, -1.0)],
@@ -194,7 +196,7 @@
         source, base, every,
         lambda i, j: [spot(1, bands, 0)(i, j, 1.0), spot(1, 0, bands)(j, i, -1.0)],
     )
-    source += second_pieces
+    source, known, entries = 0, entries, []
     for shift in range(bands // 2 + 1):
         for lane in range(width):
             i = lane // (width // bands)
@@ -207,7 +209,7 @@
                 entries.append((source + 2 * shift, lane, real_row, at, 1.0))
                 if shift:
                     entries.append((source + 2 * shift + 1, lane, imag_row, at, sign))
-    return entries
+    return known, entries
 
 
 def solve(system, size, width):
@@ -266,12 +268,15 @@
     pltpu.make_async_copy(ref, ref, sem).wait()
 
 
-def total(place, mine, first, second, sems, values):
+def total_start(place, mine, first, sems, values):
     mine[0] = values
     first[place.slab] = values
     for step in range(1, place.slabs):
         _, device = place.slab_peer(step)
         send(mine.at[0], first.at[place.slab], sems.at[0], sems.at[1], device)
+
+
+def total_turn(place, mine, first, second, sems):
     await_bytes(first.at[pl.ds(0, place.slabs - 1)], sems.at[1])
     values = first[0]
     for slab in range(1, place.slabs):
@@ -281,6 +286,9 @@
     for step in range(1, place.groups):
         _, device = place.band_peer(step)
         send(mine.at[1], second.at[place.group], sems.at[2], sems.at[3], device)
+
+
+def total_end(place, first, second, sems):
     await_bytes(second.at[pl.ds(0, place.groups - 1)], sems.at[3])
     values = second[0]
     for group in range(1, place.groups):
@@ -302,19 +310,25 @@
 
 
 def step_kernel(
-    groups, slabs, arrays, solve_sources, result_sources,
+    groups, slabs, arrays, all_sources,
     permittivity, bloch, given, *refs,
 ):
     outside, refs = (given, *refs[: arrays - 1]), refs[arrays - 1 :]
     (search, results), inside, refs = refs[:2], refs[2 : arrays + 2], refs[arrays + 2 :]
     block, materials, x_split, x_minus, y_plus, y_minus = inside[:6]
-    z_plus, z_minus = inside[6:8] if arrays == 12 else (y_plus, y_minus)
-    solve_spread, solve_gather, result_spread, result_gather = inside[-4:]
+    z_plus, z_minus = inside[6:8] if arrays == 16 else (y_plus, y_minus)
+    (
+        solve_spread, solve_gather, side_spread, side_gather,
+        known_spread, known_gather, field_spread, field_gather,
+    ) = inside[-8:]
+    solve_sources, side_sources, known_sources, field_sources = all_sources
     (
         work, image, out_y, in_z, out_z, in_y, out_x, eta, local_eta, cells, waves, depths, mixing,
-        first_acc, first_tile, first_mine, first_slab, first_band,
+        own_acc, cross_acc, first_tile, own_mine, own_slab, own_band,
+        cross_mine, cross_slab, cross_band,
         second_acc, field_acc, second_tile, second_mine, second_slab, second_band,
-        sems, comes, ends, tail, loads,
+        field_mine, field_slab, field_band, inverse,
+        sems, comes, ends, tail, paths, loads,
     ) = refs
     place = Place(groups, slabs)
     bands, _, _, depth, rows, width = block.shape
@@ -328,6 +342,9 @@
     parts = share // 8
     lead = min(WINDOW, chunks)
 
+    for place_of, (source, target) in enumerate(zip(outside, inside)):
+        pltpu.make_async_copy(source, target, loads.at[place_of]).start()
+
     enter(
         [place.slab_peer(i)[1] for i in range(1, slabs)]
         + [
@@ -336,9 +353,6 @@
             for core in range(2)
         ]
     )
-
-    for place_of, (source, target) in enumerate(zip(outside, inside)):
-        pltpu.make_async_copy(source, target, loads.at[place_of]).start()
 
     def send_out(k):
         for i in range(1, slabs):
@@ -366,15 +380,38 @@
                     values = jnp.where(found == material, permittivity[material] / cell_count, values)
                 cells[cell, pl.ds((part * thin + z) * 8, 8), :] = values
 
-    def send_cells():
-        for part in range(parts):
-            target = pl.ds((part * length + thin * place.slab) * 8, thin * 8)
-            for i in range(1, slabs):
-                slab, device = place.slab_peer(i)
+    reach = slabs // 4
+    first_layer = reach * (place.layer // reach)
+    mirror = slabs // 2 - 1 - place.layer
+
+    def near_peer(step):
+        layer = first_layer + lax.rem(place.layer - first_layer + step, reach)
+        return layer
+
+    def cell_rows(part, slab):
+        return pl.ds((part * length + thin * slab) * 8, thin * 8)
+
+    def send_cells(part, layer, core, send_sem, recv_sem):
+        send(
+            cells.at[2 * place.group + core, pl.ds(part * thin * 8, thin * 8), :],
+            eta.at[cell_rows(part, place.slab), :],
+            send_sem, recv_sem, (place.group, 2 * layer + core),
+        )
+
+    def send_near(part):
+        for i in range(1, reach):
+            for core in range(2):
+                send_cells(part, near_peer(i), core, paths.at[0, part], paths.at[1, part])
+        send_cells(part, place.layer, 1 - place.core, paths.at[0, part], paths.at[1, part])
+
+    def hand_on(part):
+        await_bytes(eta.at[pl.ds(0, 2 * thin * 8), :], paths.at[3, part])
+        for i in range(1, reach):
+            for core in range(2):
+                at = cell_rows(part, 2 * mirror + core)
                 send(
-                    cells.at[2 * place.group + slab % 2, pl.ds(part * thin * 8, thin * 8), :],
-                    eta.at[target, :],
-                    tail.at[2, part], tail.at[3, part], device,
+                    eta.at[at, :], eta.at[at, :], paths.at[4, part], paths.at[5, part],
+                    (place.group, 2 * near_peer(i) + place.core),
                 )
 
     for part in range(parts):
@@ -393,8 +430,10 @@
         at_z = jnp.broadcast_to(place.group * depth + z, (8, width))
         depths[z] = wave(length, 0.2, fraction, at_z)
 
-    first_acc[...] = jnp.zeros_like(first_acc)
-    gram(first_acc, 0, True, block, block, depth, lambda t: t)
+    own_acc[...] = jnp.zeros_like(own_acc)
+    cross_acc[...] = jnp.zeros_like(cross_acc)
+    gram(own_acc, 0, True, block, block, depth, lambda t: t)
+    total_start(place, own_mine, own_slab, tail.at[0], lane_sums(first_tile, own_acc))
 
     @pl.loop(0, chunks)
     def _(z):
@@ -406,9 +445,17 @@
         def _():
             send_out(z + lead)
 
+        for part in range(parts):
+
+            @pl.when(z == 1 + 4 * part)
+            def _(part=part):
+                send_near(part)
+
         @pl.when(z == chunks - 1)
         def _():
-            send_cells()
+            for part in range(parts):
+                for core in range(2):
+                    send_cells(part, mirror, core, paths.at[2, part], paths.at[3, part])
 
         for comp in range(2):
             for ri in range(2):
@@ -485,6 +532,7 @@
                     ri * length : (ri + 1) * length, j * width : (j + 1) * width
                 ]
 
+    hand_on(0)
     for part in range(parts):
         @pl.loop(0, chunks)
         def _(k, part=part):
@@ -495,6 +543,10 @@
             first = part * length * 8 + 2 * pair
             for c in range(3):
                 keep_columns(in_z, c, first, left_transform(z_plus, columns_of(in_z, c, first)))
+
+    for part in range(1, parts):
+        hand_on(part)
+    total_turn(place, own_mine, own_slab, own_band, tail.at[0])
 
     def send_back(k, part):
         for i in range(1, 2 * groups):
@@ -506,7 +558,9 @@
             )
 
     for part in range(parts):
-        await_bytes(eta.at[pl.ds(0, thin * 8 * (slabs - 1)), :], tail.at[3, part])
+        await_bytes(eta.at[pl.ds(0, thin * 8 * (2 * reach - 1)), :], paths.at[1, part])
+        if reach > 1:
+            await_bytes(eta.at[pl.ds(0, thin * 16 * (reach - 1)), :], paths.at[5, part])
 
         @pl.loop(0, 4)
         def _(pair, part=part):
@@ -519,8 +573,11 @@
                 field = columns_of(in_z, c, first) * weight
                 keep_columns(out_z, c, first, left_transform(z_minus, field))
 
-        @pl.loop(0, lead)
-        def _(k, part=part):
+        send_back(0, part)
+
+    @pl.loop(1, lead)
+    def _(k):
+        for part in range(parts):
             send_back(k, part)
 
     @pl.loop(0, chunks)
@@ -593,26 +650,38 @@
                 sems.at[6, z], sems.at[7, z], device,
             )
 
+    own_sums = total_end(place, own_slab, own_band, tail.at[0])
+    pieces = lambda values, row: [
+        values[row : row + 1, at : at + width] for at in range(0, values.shape[1], width)
+    ]
+    system = scatter(pieces(own_sums, 0), solve_sources, solve_spread, solve_gather)
+    rows_at = lax.broadcasted_iota(jnp.int32, system.shape, 0)
+    lanes_at = lax.broadcasted_iota(jnp.int32, system.shape, 1)
+    inverse[...] = solve(
+        jnp.where(lanes_at == rows_at + 2 * bands, 1.0, system), 2 * bands, width
+    )
+
     @pl.loop(0, chunks)
     def _(k):
         await_bytes(
             work.at[:, :, pl.ds(0, 1), pl.ds(0, rows * (slabs - 1)), :], sems.at[7, k]
         )
         gram(
-            first_acc, gram_rows(bands, True), True, block, image, 2, lambda t: half * t + k,
-        )
-
-    first_sums = total(place, first_mine, first_slab, first_band, tail.at[0], lane_sums(first_tile, first_acc))
-    pieces = lambda values, row: [
-        values[row : row + 1, at : at + width] for at in range(0, values.shape[1], width)
-    ]
-    system = solve(
-        scatter(pieces(first_sums, 0), solve_sources, solve_spread, solve_gather), 2 * bands, width
-    )
+            cross_acc, 0, True, block, image, 2, lambda t: half * t + k,
+        )
+
+    total_start(place, cross_mine, cross_slab, tail.at[1], lane_sums(first_tile, cross_acc))
+    total_turn(place, cross_mine, cross_slab, cross_band, tail.at[1])
+    cross_sums = total_end(place, cross_slab, cross_band, tail.at[1])
+    side = scatter(pieces(cross_sums, 0), side_sources, side_spread, side_gather)
+    factors = inverse[...]
+    system = factors[:, 2 * bands : 2 * bands + 1] * side[0:1, :]
+    for k in range(1, 2 * bands):
+        system += factors[:, 2 * bands + k : 2 * bands + k + 1] * side[k : k + 1, :]
     for row in range(2 * bands):
         for j in range(bands):
             mixing[row, j] = jnp.broadcast_to(
-                system[row : row + 1, 2 * bands + j : 2 * bands + j + 1], (8, width)
+                system[row : row + 1, j : j + 1], (8, width)
             )
 
     @pl.loop(0, chunks)
@@ -625,7 +694,10 @@
         await_bytes(slab_bytes, sems.at[6, k])
 
     for part in range(parts):
-        await_bytes(eta.at[pl.ds(0, thin * 8 * (slabs - 1)), :], tail.at[2, part])
+        await_bytes(eta.at[pl.ds(0, thin * 8 * (2 * reach - 1)), :], paths.at[0, part])
+        await_bytes(eta.at[pl.ds(0, thin * 16), :], paths.at[2, part])
+        if reach > 1:
+            await_bytes(eta.at[pl.ds(0, thin * 16 * (reach - 1)), :], paths.at[4, part])
 
     quarter = width // groups
     second_acc[...] = jnp.zeros_like(second_acc)
@@ -633,15 +705,19 @@
     lane = lax.broadcasted_iota(jnp.int32, (1, width), 1) // quarter
     deep_step = 8 if depth % 8 == 0 else 1
 
-    def send_quarter(k):
+    def send_rows(k, first, count):
         part, c = k // 3, k % 3
+        base = (part * length + depth * place.group) * 8
         for i in range(1, groups):
             group, device = place.band_peer(i)
             send(
-                out_x.at[part * groups + group, c],
-                in_z.at[c, :, pl.ds((part * length + depth * place.group) * 8, depth * 8), :],
+                out_x.at[part * groups + group, c, :, pl.ds(first, count), :],
+                in_z.at[c, :, pl.ds(base + first, count), :],
                 ends.at[0, k], ends.at[1, k], device,
             )
+
+    def send_quarter(k):
+        send_rows(k, 0, depth * 8)
 
     @pl.loop(0, parts)
     def _(part):
@@ -650,25 +726,25 @@
             waves[i, pl.ds(rows * place.slab + part * 8, 8), :] for i in range(3)
         )
 
-        @pl.loop(0, depth)
-        def _(z):
-            tile_at = (z, band_rows, slice(None))
-            deep = depths[z]
-            scale = 1.0 / (planar * planar + deep * deep + 1.0)
-            for comp in range(2):
-                reals = [block[(i, comp, 0) + tile_at] for i in range(bands)]
-                imags = [block[(i, comp, 1) + tile_at] for i in range(bands)]
-                for j in range(bands):
-                    real = image[(j, comp, 0) + tile_at]
-                    imag = image[(j, comp, 1) + tile_at]
-                    for i in range(bands):
-                        real = real - (reals[i] * mixing[i, j] - imags[i] * mixing[bands + i, j])
-                        imag = imag - (reals[i] * mixing[bands + i, j] + imags[i] * mixing[i, j])
-                    search[(j, comp, 0) + tile_at] = real * scale
-                    search[(j, comp, 1) + tile_at] = imag * scale
-
         @pl.loop(0, depth // deep_step)
         def _(group):
+            @pl.loop(group * deep_step, (group + 1) * deep_step)
+            def _(z):
+                tile_at = (z, band_rows, slice(None))
+                deep = depths[z]
+                scale = 1.0 / (planar * planar + deep * deep + 1.0)
+                for comp in range(2):
+                    reals = [block[(i, comp, 0) + tile_at] for i in range(bands)]
+                    imags = [block[(i, comp, 1) + tile_at] for i in range(bands)]
+                    for j in range(bands):
+                        real = image[(j, comp, 0) + tile_at]
+                        imag = image[(j, comp, 1) + tile_at]
+                        for i in range(bands):
+                            real = real - (reals[i] * mixing[i, j] - imags[i] * mixing[bands + i, j])
+                            imag = imag - (reals[i] * mixing[bands + i, j] + imags[i] * mixing[i, j])
+                        search[(j, comp, 0) + tile_at] = real * scale
+                        search[(j, comp, 1) + tile_at] = imag * scale
+
             planes = pl.ds(group * deep_step, deep_step)
             deep = depths[planes]
             size = jnp.sqrt(planar * planar + deep * deep)
@@ -706,15 +782,15 @@
                     for c in range(3):
                         out_x[part * groups + target, c, ri, at, :] = packed[c * count : (c + 1) * count]
 
+            @pl.when(part == 0)
+            def _():
+                send_rows(0, group * count, count)
+
         for c in range(3):
             for ri in range(2):
                 in_z[c, ri, pl.ds((part * length + depth * place.group) * 8, depth * 8), :] = out_x[
                     part * groups + place.group, c, ri
                 ]
-
-        @pl.when(part == 0)
-        def _():
-            send_quarter(0)
 
     @pl.loop(0, 3 * parts)
     def _(k):
@@ -764,6 +840,20 @@
     base = gram(second_acc, 0, False, block, search, depth, lambda t: t)
     base = gram(second_acc, base, True, search, search, depth, lambda t: t)
     gram(second_acc, base, False, search, image, depth, lambda t: t)
+    total_start(place, second_mine, second_slab, tail.at[2], lane_sums(second_tile, second_acc))
+
+    def add_products(real, imag, weight):
+        real_weighted, imag_weighted = real * weight, imag * weight
+        for shift in range(bands // 2 + 1):
+            if shift == 0:
+                real_other, imag_other = real, imag
+            else:
+                real_other = pltpu.roll(real, quarter * shift, 1)
+                imag_other = pltpu.roll(imag, quarter * shift, 1)
+            real_term = real_weighted * real_other + imag_weighted * imag_other
+            imag_term = real_weighted * imag_other - imag_weighted * real_other
+            for place_of, term in ((2 * shift, real_term), (2 * shift + 1, imag_term)):
+                field_acc[place_of] += jnp.sum(term.reshape(height // 8, 8, width), axis=0)
 
     for c in range(3):
         for part in range(parts):
@@ -772,46 +862,40 @@
                 ends.at[3, part * 3 + c],
             )
 
-        @pl.loop(0, thin)
-        def _(z, c=c):
+        @pl.loop(0, thin // 2)
+        def _(pair, c=c):
             stacked = jnp.concatenate(
                 [
-                    in_y[slab, c, ri, pl.ds(part * thin * 8 + 8 * z, 8), :]
-                    for ri in range(2)
-                    for slab in range(slabs)
-                    for part in range(parts)
+                    jnp.concatenate(
+                        [
+                            in_y[slab, c, ri, pl.ds(part * thin * 8 + 16 * pair + 8 * j, 8), :]
+                            for ri in range(2)
+                            for slab in range(slabs)
+                            for part in range(parts)
+                        ],
+                        0,
+                    )
+                    for j in range(2)
                 ],
-                0,
+                1,
             )
-            field = left_transform(y_plus, stacked)
-            real, imag = field[:height], field[height:]
-            weight = local_eta[z]
-            real_weighted, imag_weighted = real * weight, imag * weight
-            for shift in range(bands // 2 + 1):
-                if shift == 0:
-                    real_other, imag_other = real, imag
-                else:
-                    real_other = pltpu.roll(real, quarter * shift, 1)
-                    imag_other = pltpu.roll(imag, quarter * shift, 1)
-                real_term = real_weighted * real_other + imag_weighted * imag_other
-                imag_term = real_weighted * imag_other - imag_weighted * real_other
-                for place_of, term in ((2 * shift, real_term), (2 * shift + 1, imag_term)):
-                    field_acc[place_of] += jnp.sum(term.reshape(height // 8, 8, width), axis=0)
+            planes = left_transform(y_plus, stacked)
+            for j in range(2):
+                lanes = slice(j * width, (j + 1) * width)
+                add_products(planes[:height, lanes], planes[height:, lanes], local_eta[2 * pair + j])
 
     fields = jnp.sum(field_acc[...], axis=1)
     fields = pltpu.roll(fields, lax.rem(width - quarter * place.group, width), 1)
-    values = lane_sums(second_tile, second_acc)
-    if values.shape[1] > width:
-        empty = jnp.zeros((fields.shape[0], values.shape[1] - width), jnp.float32)
-        fields = jnp.concatenate([fields, empty], 1)
-    second_sums = total(
-        place, second_mine, second_slab, second_band, tail.at[1],
-        jnp.concatenate([values, fields], 0),
-    )
-    listed = pieces(first_sums, 0) + pieces(second_sums, 0)
-    for row in range(2 * (bands // 2 + 1)):
-        listed.append(second_sums[8 + row : 9 + row, :width])
-    results[...] = scatter(listed, result_sources, result_spread, result_gather) / cell_count
+    total_start(place, field_mine, field_slab, tail.at[3], fields)
+    total_turn(place, second_mine, second_slab, second_band, tail.at[2])
+    total_turn(place, field_mine, field_slab, field_band, tail.at[3])
+    second_sums = total_end(place, second_slab, second_band, tail.at[2])
+    listed = pieces(own_sums, 0) + pieces(cross_sums, 0) + pieces(second_sums, 0)
+    known = scatter(listed, known_sources, known_spread, known_gather)
+    fields = total_end(place, field_slab, field_band, tail.at[3])
+    listed = [fields[row : row + 1] for row in range(2 * (bands // 2 + 1))]
+    fields = scatter(listed, field_sources, field_spread, field_gather)
+    results[...] = (known + fields) / cell_count
 
     @pl.loop(0, 3 * parts)
     def _(k):
@@ -833,12 +917,11 @@
     share = height // (2 * groups)
     thin, parts, quarter = length // slabs, rows // 8, width // groups
     chunks = half
-    first_count = 2 * gram_rows(bands, True)
+    first_count = gram_rows(bands, True)
     first_lanes = round_up(first_count, width)
     second_count = 2 * gram_rows(bands, False) + gram_rows(bands, True)
     second_lanes = round_up(second_count, width)
     field_rows = round_up(2 * (bands // 2 + 1), 8)
-    message = (8 + field_rows, second_lanes)
 
     plain = dft_matrix(width, 1.0).T
     orders = []
@@ -847,27 +930,31 @@
         source = ((spots - band) % groups) * quarter + np.arange(width) % quarter
         orders.append(right_table(plain[:, np.concatenate([source, width + source])]))
     first_pieces, second_pieces = first_lanes // width, second_lanes // width
-    solve_sources, *solve_tables = scatter_tables(system_entries(bands), first_pieces, width)
-    result_sources, *result_tables = scatter_tables(
-        result_entries(bands, width, first_pieces, second_pieces),
-        first_pieces + second_pieces + 2 * (bands // 2 + 1),
-        width,
-    )
+    known, fields = result_entries(bands, width, first_pieces, second_pieces)
+    scattered = [
+        scatter_tables(entries, count, width)
+        for entries, count in (
+            (system_entries(bands), first_pieces),
+            (side_entries(bands), first_pieces),
+            (known, 2 * first_pieces + second_pieces),
+            (fields, 2 * (bands // 2 + 1)),
+        )
+    ]
     tables = [
         np.stack(orders),
         right_table(dft_matrix(width, -1.0).T),
         left_table(height, 1.0),
         left_table(height, -1.0),
         *([] if length == height else [left_table(length, 1.0), left_table(length, -1.0)]),
-        *solve_tables,
-        *result_tables,
+        *[table for _, *pair in scattered for table in pair],
     ]
     single = lambda *shape: pltpu.VMEM(shape, jnp.float32)
+    slots = lambda *tile: [single(2, *tile), single(slabs, *tile), single(groups, *tile)]
     by_cell = (2 * groups, 3, 2, half * share, width)
     by_part = (parts * groups, 3, 2, depth * 8, width)
     out_x = [] if by_cell == by_part else [single(*by_part)]
     kernel = partial(
-        step_kernel, groups, slabs, 2 + len(tables), solve_sources, result_sources
+        step_kernel, groups, slabs, 2 + len(tables), [sources for sources, *_ in scattered]
     )
 
     def body(*refs):
@@ -883,7 +970,7 @@
         out_specs=vmem(2),
         out_shape=[
             pltpu.VMEM(block.shape, jnp.float32),
-            jax.ShapeDtypeStruct((result_tables[0].shape[0], width), jnp.float32),
+            jax.ShapeDtypeStruct((8 * bands, width), jnp.float32),
         ],
         scratch_shapes=[
             *[pltpu.VMEM(array.shape, array.dtype) for array in (block, materials, *tables)],
@@ -901,20 +988,21 @@
             single(depth, 8, width),
             single(2 * bands, bands, 8, width),
             single(first_count, 8, width),
+            single(first_count, 8, width),
             single(first_lanes, width),
-            single(2, 8, first_lanes),
-            single(slabs, 8, first_lanes),
-            single(groups, 8, first_lanes),
+            *slots(8, first_lanes),
+            *slots(8, first_lanes),
             single(second_count, 8, width),
             single(field_rows, 8, width),
             single(second_lanes, width),
-            single(2, *message),
-            single(slabs, *message),
-            single(groups, *message),
+            *slots(8, second_lanes),
+            *slots(field_rows, width),
+            single(2 * bands, width),
             pltpu.SemaphoreType.DMA((8, chunks)),
             pltpu.SemaphoreType.DMA((parts, chunks)),
             pltpu.SemaphoreType.DMA((4, 3 * parts)),
             pltpu.SemaphoreType.DMA((4, 4)),
+            pltpu.SemaphoreType.DMA((6, parts)),
             pltpu.SemaphoreType.DMA((2 + len(tables),)),
         ],
         compiler_params=pltpu.CompilerParams(

time: 401 us -> 394 us (0.983)
  Pallas kernels: 397 us -> 390 us
    pallas_call x1, Pallas kernels: 397 us -> 390 us  [step(): pl.pallas_call(body, in_specs=[pl.BlockSpec(memory_space=pltpu.SMEM)] * 2...]
where the time goes in v4:
time: 394 us
  Pallas kernels  390 us (99%)
    pallas_call x1, Pallas kernels, step(): pl.pallas_call(body, in_specs=[pl.BlockSpec(memory_space=pltpu.SMEM)] * 2...  390 us

profile of v4, /device:TPU:0, one launch (start us, length us, event | category | flops | bytes accessed | tf_op | source)
XLA Modules:
  0.0 393.6 jit_solution(2973866458780404325)
XLA Ops:
  1.3 389.7 %shard_map.175 = (f32[4,2,2,32,16,128]{5,4,3,2,1,0:T(8,128)S(1)}, f32[32,128]{1,0:T(8,128)}) custom-call(f32[4]{0:T(128)} %refs_0_.1, s32[1]{0:T(128)S(6)} %copy.27.refs_1_, f32[4,2,2,32,16,128]{5,4,3,2,1,0:T(8,128)} %refs_2_.1, s32[16,128,128]{2,1,0:T(8,128)} %refs_3_.1, bf16[4,512,256]{2,1,0:T(8,128)(2,1)} %constant.22.clone.refs_4_, ...), custom_call_target="tpu_custom_call" | custom-call | tf_op jit(solution)/shard_map/pallas_call | solution.py:967
  391.0 0.0 copy-start
  391.0 2.0 copy.26
  393.0 0.0 copy-done
  393.0 0.6 slice_bitcast_fusion
Async XLA Ops:
  391.0 2.0 copy-start

commit v5 on v4

--- a/solution.py
+++ b/solution.py
@@ -13,7 +13,7 @@
 HIGHEST = lax.Precision.HIGHEST
 MESH = pl.DeviceIdType.MESH
 VMEM_LIMIT = 54 * 1024 * 1024
-WINDOW = 3
+WINDOW = 2
 
 
 def halves(values):
@@ -451,9 +451,10 @@
             def _(part=part):
                 send_near(part)
 
-        @pl.when(z == chunks - 1)
-        def _():
-            for part in range(parts):
+        for part in range(parts):
+
+            @pl.when(z == chunks - parts + part)
+            def _(part=part):
                 for core in range(2):
                     send_cells(part, mirror, core, paths.at[2, part], paths.at[3, part])
 

time: 394 us -> 390 us (0.990)
  Pallas kernels: 390 us -> 386 us
where the time goes in v5:
time: 390 us
  Pallas kernels  386 us (99%)
    pallas_call x1, Pallas kernels, step(): pl.pallas_call(body, in_specs=[pl.BlockSpec(memory_space=pltpu.SMEM)] * 2...  386 us

profile of v5, /device:TPU:0, one launch (start us, length us, event | category | flops | bytes accessed | tf_op | source)
XLA Modules:
  0.0 389.9 jit_solution(9997669014975756405)
XLA Ops:
  1.3 386.0 %shard_map.175 = (f32[4,2,2,32,16,128]{5,4,3,2,1,0:T(8,128)S(1)}, f32[32,128]{1,0:T(8,128)}) custom-call(f32[4]{0:T(128)} %refs_0_.1, s32[1]{0:T(128)S(6)} %copy.27.refs_1_, f32[4,2,2,32,16,128]{5,4,3,2,1,0:T(8,128)} %refs_2_.1, s32[16,128,128]{2,1,0:T(8,128)} %refs_3_.1, bf16[4,512,256]{2,1,0:T(8,128)(2,1)} %constant.22.clone.refs_4_, ...), custom_call_target="tpu_custom_call" | custom-call | tf_op jit(solution)/shard_map/pallas_call | solution.py:968
  387.3 0.0 copy-start
  387.3 2.0 copy.26
  389.3 0.0 copy-done
  389.3 0.6 slice_bitcast_fusion
Async XLA Ops:
  387.3 2.0 copy-start
